TPU v7x, 256 devices: a whole 4x4x8 slice. The times are simulated.
256 devices in a mesh: grp: 8 (over x, core), dev: 32 (over z, y).
Axes of the slice: x: 4, y: 4, z: 8, core: 2. Of those that a mesh axis runs over, the one named last changes fastest.
Arguments:
- points: bfloat16 [524288, 1024], P(('grp', 'dev')), may hold values from -6 to 6
- blocks: int32 [524288, 1], P(('grp', 'dev')), may hold values from 0 to 255; in each aligned block of 2048 rows (0 to 2047, 2048 to 4095, ...) at most 16 rows name the same one
- finals: int32 [524288], P(('grp', 'dev')), may hold values from 0 to 255
- centroids: bfloat16 [65536, 1024], P('dev'), may hold values from -6 to 6
Outputs:
- distances: bfloat16 [524288, 256], P(('grp', 'dev'))
- refreshed_centroids: float32 [65536, 1024], P('dev', 'grp')
Inputs may be any that keep to these rules, and one draw needn't show every extreme that they name: `blocks`: among the 2048 rows of one device no block is named by more than 16 rows, and some block by exactly 16. Block b is held by index b // 8 of dev. The point's centroid is row 256 * blocks + finals of centroids.
All inputs are finite; a program needn't handle non-finite values.
Results may differ from a plain program's by a relative error of at most 0.008.
Values may be sent and summed in bfloat16 or wider, within the bound.
No kernel may reach another device: no remote copies, remote signals or barrier semaphores. Data moves between devices by JAX's collectives and lax.ppermute only.
A program may use at most 128 MiB of HBM per device.

v0:
```python
import functools

import jax
import jax.numpy as jnp
from jax import lax
from jax.experimental import pallas as pl
from jax.experimental.pallas import tpu as pltpu
from jax.sharding import Mesh
from jax.sharding import PartitionSpec as P

BS = 256
MOST = 16
NX, NC, NZ, NY = 4, 2, 8, 4
NG = NX * NC
NB = NZ * NY * NG
DESTS = NG * NY
SLOTS = NZ * MOST
WIDTHS = (384, 384, 256)
PLANE = ("x", "c", "y")
DIGIT = 64
GRANT = 32 * 2**20
PAIR = 2
PER_STEP = 4
F32, BF16 = jnp.float32, jnp.bfloat16


def mask(where):
    return jnp.where(where, jnp.ones((), BF16), jnp.zeros((), BF16))


def nt_dot(a, b):
    return lax.dot_general(a, b, (((1,), (1,)), ((), ())), preferred_element_type=F32)


def slots_of(block_row):
    npts = block_row.shape[1]
    piece = 128
    row = lax.broadcasted_iota(jnp.int32, (piece, 2 * piece), 0)
    column = lax.broadcasted_iota(jnp.int32, (piece, 2 * piece), 1)
    before = jnp.where((row < column) | (column >= piece), 1.0, 0.0).astype(BF16)
    carry = jnp.zeros((NB, piece), F32)
    ranks = []
    for i in range(npts // piece):
        part = block_row[:, i * piece : (i + 1) * piece]
        member = lax.broadcasted_iota(jnp.int32, (NB, piece), 0) == part
        ones = jnp.where(member, 1.0, 0.0)
        seen = jnp.dot(ones.astype(BF16), before, preferred_element_type=F32)
        ranks.append(jnp.sum(ones * (seen[:, :piece] + carry), axis=0, keepdims=True))
        carry = carry + seen[:, piece:]
    rank = jnp.concatenate(ranks, axis=1).astype(jnp.int32)
    zz = block_row // (NY * NG)
    yy = (block_row // NG) % NY
    gg = block_row % NG
    return ((gg * NY + yy) * NZ + zz) * MOST + rank


def low_digits(slots):
    line = lax.broadcasted_iota(jnp.int32, (DIGIT, slots.shape[1]), 0)
    return jnp.where(line == slots % DIGIT, 1.0, 0.0).astype(BF16)


def pick_rows(slots, low, base, rows):
    npts = slots.shape[1]
    line = lax.broadcasted_iota(jnp.int32, (rows // DIGIT, npts), 0)
    high = jnp.where(line + base // DIGIT == slots // DIGIT, 1.0, 0.0)
    parts = []
    for i in range(rows // DIGIT):
        one = jnp.broadcast_to(high[i : i + 1], (16, npts)).astype(BF16)
        parts.append(low * jnp.concatenate([one] * (DIGIT // 16), axis=0))
    return jnp.concatenate(parts, axis=0)


def first_prep(block_ref, final_ref, points_ref, out_ref, slot_ref, slots, low, targets):
    step = pl.program_id(0)

    @pl.when(step == 0)
    def _():
        found = slots_of(block_ref[...])
        slots[...] = found
        slot_ref[...] = found
        low[...] = low_digits(found)
        line = lax.broadcasted_iota(jnp.int32, (DESTS * SLOTS // DIGIT, found.shape[1]), 0)
        high = jnp.where(line == found // DIGIT, (final_ref[...] + 1).astype(F32), 0.0)
        targets[...] = nt_dot(high.astype(BF16), low[...])

    rows = PER_STEP * SLOTS
    width = points_ref.shape[1]
    pick = pick_rows(slots[...], low[...], step * rows, rows)
    moved = jnp.dot(pick, points_ref[...], preferred_element_type=F32)
    out_ref[:, 0:SLOTS] = moved.astype(BF16).reshape(PER_STEP, SLOTS, width)
    digits = rows // DIGIT
    target = targets[pl.ds(pl.multiple_of(step * digits, digits), digits)]
    blank = jnp.zeros((1, width - SLOTS), F32)
    for i in range(PER_STEP):
        each = SLOTS // DIGIT
        one = [target[j : j + 1] for j in range(i * each, (i + 1) * each)]
        one = jnp.concatenate(one + [blank], axis=1)
        out_ref[i, SLOTS : SLOTS + 8] = jnp.broadcast_to(one, (8, width)).astype(BF16)


def later_prep(slot_ref, points_ref, out_ref, low):
    step = pl.program_id(0)

    @pl.when(step == 0)
    def _():
        low[...] = low_digits(slot_ref[...])

    rows = PER_STEP * SLOTS
    pick = pick_rows(slot_ref[...], low[...], step * rows, rows)
    moved = jnp.dot(pick, points_ref[...], preferred_element_type=F32)
    out_ref[...] = moved.astype(BF16).reshape(out_ref.shape)


def prepare(block_row, final_row, points, start, width, slot_row):
    npts = points.shape[0]
    steps = DESTS // PER_STEP
    column = start // width
    whole = pl.BlockSpec((1, npts), lambda i: (0, 0))
    point_spec = pl.BlockSpec((npts, width), lambda i: (0, column))
    tall = SLOTS if slot_row is not None else SLOTS + 8
    out_spec = pl.BlockSpec((PER_STEP, tall, width), lambda i: (i, 0, 0))
    out_shape = jax.ShapeDtypeStruct((DESTS, tall, width), BF16)
    cost = pl.CostEstimate(
        flops=2 * DESTS * SLOTS * npts * width,
        bytes_accessed=2 * width * (npts + DESTS * SLOTS),
        transcendentals=0,
    )
    if slot_row is not None:
        return pl.pallas_call(
            later_prep,
            grid=(steps,),
            in_specs=[whole, point_spec],
            out_specs=out_spec,
            out_shape=out_shape,
            scratch_shapes=[pltpu.VMEM((DIGIT, npts), BF16)],
            cost_estimate=cost,
        )(slot_row, points)
    return pl.pallas_call(
        first_prep,
        grid=(steps,),
        in_specs=[whole, whole, point_spec],
        out_specs=(out_spec, whole),
        out_shape=(out_shape, jax.ShapeDtypeStruct((1, npts), jnp.int32)),
        scratch_shapes=[
            pltpu.VMEM((1, npts), jnp.int32),
            pltpu.VMEM((DIGIT, npts), BF16),
            pltpu.VMEM((DESTS * SLOTS // DIGIT, DIGIT), F32),
        ],
        cost_estimate=cost,
    )(block_row, final_row, points)


def work_kernel(first, last, me_ref, *refs):
    refs = list(refs)
    rows_ref, target_ref = refs[:2]
    piece_refs = refs[2 : 2 + NZ]
    part_ref = None if first else refs[2 + NZ]
    sum_refs, result_ref, tables, packs = refs[-NZ - 3 : -3], refs[-3], refs[-2], refs[-1]
    places = [
        lax.rem(me_ref[0] - (pl.program_id(0) * PAIR + b) + NZ, NZ) for b in range(PAIR)
    ]
    for b in range(PAIR):
        for i in range(NZ):

            @pl.when(places[b] == i)
            def _(b=b, i=i):
                tables[b] = piece_refs[i][...]

    for b in range(PAIR):
        rows = rows_ref[:, b * MOST : (b + 1) * MOST, :].reshape(DESTS * MOST, rows_ref.shape[-1])
        table = tables[b]
        onehot = jnp.where(
            lax.broadcasted_iota(jnp.int32, (BS, DESTS * MOST), 0) == target_ref[b], 1.0, 0.0
        ).astype(BF16)
        sums = jnp.dot(onehot, rows, preferred_element_type=F32)
        packs[b, 0:BS] = sums.astype(BF16)
        if first:
            ones = jnp.ones((8, DESTS * MOST), BF16)
            count = nt_dot(ones, onehot)
            high = jnp.floor(count * (1.0 / 16.0))
            low = count - 16.0 * high
            which = lax.broadcasted_iota(jnp.int32, count.shape, 0)
            digits = jnp.where(which == 0, low, jnp.where(which == 1, high, 0.0))
            blank = jnp.zeros((8, sums.shape[1] - BS), F32)
            packs[b, BS : BS + 8] = jnp.concatenate([digits, blank], axis=1).astype(BF16)
        cross = nt_dot(rows, table)
        wide = rows.astype(F32)
        row_norm = jnp.sum(wide * wide, axis=1, keepdims=True)
        tall = table.astype(F32)
        cent_norm = jnp.sum(tall * tall, axis=1, keepdims=True)
        cent_norm = jnp.transpose(jnp.broadcast_to(cent_norm, (BS, 128)))[0:1]
        total = row_norm - 2.0 * cross + cent_norm
        if not first:
            total = total + part_ref[b]
        if last:
            total = (total * (1.0 / 1024.0)).astype(BF16)
            result_ref[:, b * MOST : (b + 1) * MOST, :] = total.reshape(DESTS, MOST, BS)
        else:
            result_ref[b] = total
    for b in range(PAIR):
        for i in range(NZ):

            @pl.when(places[b] == i)
            def _(b=b, i=i):
                sum_refs[i][...] = packs[b]


def block_work(me, rows, pieces, target, part, start, last):
    width = rows.shape[-1]
    first = part is None
    taken = DESTS * MOST
    tall = BS + 8 if first else BS
    row_spec = pl.BlockSpec((DESTS, PAIR * MOST, width), lambda k, me: (0, k, 0))
    part_spec = pl.BlockSpec((PAIR, taken, BS), lambda k, me: (k, 0, 0))
    in_specs = [row_spec, pl.BlockSpec((PAIR, 1, taken), lambda k, me: (k, 0, 0))]
    in_specs += [pl.BlockSpec((BS, width), lambda k, me: (0, start // width))] * NZ
    operands = [rows, target, *pieces]
    if not first:
        in_specs.append(part_spec)
        operands.append(part)
    if last:
        result_spec = pl.BlockSpec((DESTS, PAIR * MOST, BS), lambda k, me: (0, k, 0))
        result_shape = jax.ShapeDtypeStruct((DESTS, SLOTS, BS), BF16)
    else:
        result_spec = part_spec
        result_shape = jax.ShapeDtypeStruct((NZ, taken, BS), F32)
    return pl.pallas_call(
        functools.partial(work_kernel, first, last),
        grid_spec=pltpu.PrefetchScalarGridSpec(
            num_scalar_prefetch=1,
            grid=(NZ // PAIR,),
            in_specs=in_specs,
            out_specs=(pl.BlockSpec((tall, width), lambda k, me: (0, 0)),) * NZ + (result_spec,),
            scratch_shapes=[
                pltpu.VMEM((PAIR, BS, width), BF16),
                pltpu.VMEM((PAIR, tall, width), BF16),
            ],
        ),
        out_shape=(jax.ShapeDtypeStruct((tall, width), BF16),) * NZ + (result_shape,),
        cost_estimate=pl.CostEstimate(
            flops=4 * NZ * taken * BS * width,
            bytes_accessed=2 * width * NZ * (taken + 2 * BS) + 8 * NZ * taken * BS,
            transcendentals=0,
        ),
    )(me, *operands)


def return_kernel(slot_ref, returned_ref, out_ref):
    rows = out_ref.shape[0]
    lane = 128
    slot = jnp.transpose(jnp.broadcast_to(slot_ref[...].astype(F32), (lane, rows)))
    slot = slot.astype(jnp.int32)
    hit = slot % lane == lax.broadcasted_iota(jnp.int32, (rows, lane), 1)
    high = jnp.where(hit, slot // lane, -1).astype(F32).astype(BF16)
    total = jnp.zeros(out_ref.shape, F32)
    part = 1024
    for at in range(0, returned_ref.shape[0], part):
        pick = [mask(high == jnp.asarray(i // lane, BF16)) for i in range(at, at + part, lane)]
        pick = jnp.concatenate(pick, axis=1)
        total += jnp.dot(pick, returned_ref[at : at + part], preferred_element_type=F32)
    out_ref[...] = total.astype(BF16)


def pick_back(slot_row, returned):
    npts = slot_row.shape[1]
    rows = 512
    return pl.pallas_call(
        return_kernel,
        grid=(npts // rows,),
        in_specs=[
            pl.BlockSpec((1, rows), lambda i: (0, i)),
            pl.BlockSpec(returned.shape, lambda i: (0, 0)),
        ],
        out_specs=pl.BlockSpec((rows, BS), lambda i: (i, 0)),
        out_shape=jax.ShapeDtypeStruct((npts, BS), BF16),
        compiler_params=pltpu.CompilerParams(vmem_limit_bytes=GRANT),
        cost_estimate=pl.CostEstimate(
            flops=2 * npts * returned.shape[0] * BS,
            bytes_accessed=2 * BS * (npts + returned.shape[0]),
            transcendentals=0,
        ),
    )(slot_row, returned)


def exchange(values, axes):
    return lax.all_to_all(values, axes, split_axis=0, concat_axis=0, tiled=True)


def pass_on(values, distance):
    return lax.ppermute(values, "z", [(i, (i + distance) % NZ) for i in range(NZ)])


def gather_table(own):
    up, down, below, above = own, own, [], []
    for step in range(1, NZ // 2 + 1):
        up = pass_on(up, 1)
        below.append(up)
        if step < NZ // 2:
            down = pass_on(down, -1)
            above.append(down)
    return [own, *below, *reversed(above)]


def sum_over_planes(sums):
    total = sums[0].astype(F32)
    for k in sorted(range(1, NZ), key=lambda k: -min(k, NZ - k)):
        total = total + pass_on(sums[k], -k).astype(F32)
    return total


def shards(points, blocks, finals, centroids):
    npts, _ = points.shape
    group = lax.axis_index("x") * NC + lax.axis_index("c")
    me = lax.axis_index("z").astype(jnp.int32).reshape(1)
    own = lax.dynamic_slice_in_dim(centroids, group * BS, BS, 0)
    pieces = gather_table(own)

    block_row = blocks.reshape(1, npts)
    final_row = finals.reshape(1, npts)
    last = len(WIDTHS) - 1
    starts = [sum(WIDTHS[:i]) for i in range(last + 1)]
    arrived, slot_row = [], None
    for i, size in enumerate(WIDTHS):
        sent = prepare(block_row, final_row, points, starts[i], size, slot_row)
        if i == 0:
            sent, slot_row = sent
        arrived.append(exchange(sent, PLANE))
    target = arrived[0][:, SLOTS, :SLOTS].astype(jnp.int32) - 1
    target = jnp.transpose(target.reshape(DESTS, NZ, MOST), (1, 0, 2))
    target = target.reshape(NZ, 1, DESTS * MOST)
    part, shares = None, []
    for i in range(last + 1):
        *sums, part = block_work(
            me, arrived[i], pieces, target, part, starts[i], i == last
        )
        shares.append(sum_over_planes(sums))
    returned = exchange(part, PLANE).reshape(DESTS * SLOTS, BS)
    distances = pick_back(slot_row, returned)

    counts = shares[0][BS, :BS] + 16.0 * shares[0][BS + 1, :BS]
    total = jnp.concatenate([s[:BS] for s in shares], axis=1)
    fresh = (total + own.astype(F32)) / (counts + 1.0)[:, None]
    fresh = lax.all_to_all(fresh.astype(BF16), ("x", "c"), split_axis=1, concat_axis=0, tiled=True)
    return distances, fresh.astype(F32)


def solution(mesh):
    split = Mesh(mesh.devices.reshape(NX, NC, NZ, NY), ("x", "c", "z", "y"))
    every = ("x", "c", "z", "y")
    placed = (P(every, None), P(every, None), P(every), P(("z", "y"), None))
    return jax.shard_map(
        shards,
        mesh=split,
        in_specs=placed,
        out_specs=(P(every, None), P(("z", "y"), ("x", "c"))),
        check_vma=False,
    )
```

profile of v0, /device:TPU:1, one launch (start us, length us, event | category | flops | bytes accessed | tf_op | source)
XLA Modules:
  0.0 350.6 jit_solution(17326905427030254120)
XLA Ops:
  0.6 13.5 %shard_map.59 = (bf16[32,136,384]{2,1,0:T(8,128)(2,1)}, s32[1,2048]{1,0:T(1,128)}) custom-call(s32[1,2048]{1,0:T(1,128)} %bitcast.20, s32[1,2048]{1,0:T(1,128)} %bitcast.21, bf16[2048,1024]{1,0:T(8,128)(2,1)} %points_ref.5), custom_call_target="tpu_custom_call" | custom-call | flops 6442450944 | bytes 4718592 | tf_op jit(solution)/shard_map/pallas_call | solution.py:138
  14.1 12.4 %shard_map.61 = bf16[32,128,384]{2,1,0:T(8,128)(2,1)} custom-call(s32[1,2048]{1,0:T(1,128)} %get-tuple-element.31.slot_ref, bf16[2048,1024]{1,0:T(8,128)(2,1)} %points_ref.5), custom_call_target="tpu_custom_call" | custom-call | flops 6442450944 | bytes 4718592 | tf_op jit(solution)/shard_map/pallas_call | solution.py:129
  26.5 47.4 %all_to_all.33.refs_0_ = bf16[32,128,384]{2,1,0:T(8,128)(2,1)} all-to-all(bf16[32,128,384]{2,1,0:T(8,128)(2,1)} %shard_map.61), channel_id=1, replica_groups=mesh['x'=4,'c'=2,'z'=8,'y'=4] {'x','c','y'}, dimensions={0} | all-to-all | bytes 6291456 | tf_op jit(solution)/shard_map/all_to_all | solution.py:286
  73.9 4.8 %all-to-all-start.1 = ((bf16[32,136,384]{2,1,0:T(8,128)(2,1)}), bf16[32,136,384]{2,1,0:T(8,128)(2,1)S(1)}, u32[]{:S(2)}, u32[]{:S(2)}) async-start(bf16[32,136,384]{2,1,0:T(8,128)(2,1)} %get-tuple-element.32), calls=%async_computation.1 | async-start | bytes 6684672 | tf_op jit(solution)/shard_map/all_to_all | solution.py:286
  82.3 7.8 %shard_map.60 = bf16[32,128,256]{2,1,0:T(8,128)(2,1)} custom-call(s32[1,2048]{1,0:T(1,128)} %get-tuple-element.31.slot_ref, bf16[2048,1024]{1,0:T(8,128)(2,1)} %points_ref.5), custom_call_target="tpu_custom_call" | custom-call | flops 4294967296 | bytes 3145728 | tf_op jit(solution)/shard_map/pallas_call | solution.py:129
  90.1 29.5 %all-to-all-done.1.refs_0_ = bf16[32,136,384]{2,1,0:T(8,128)(2,1)S(1)} async-done(((bf16[32,136,384]{2,1,0:T(8,128)(2,1)}), bf16[32,136,384]{2,1,0:T(8,128)(2,1)S(1)}, u32[]{:S(2)}, u32[]{:S(2)}) %all-to-all-start.1) | async-done | bytes 3342368 | tf_op jit(solution)/shard_map/all_to_all | solution.py:286
  119.5 7.2 %all-to-all-start = ((bf16[32,128,256]{2,1,0:T(8,128)(2,1)}), bf16[32,128,256]{2,1,0:T(8,128)(2,1)}, u32[]{:S(2)}, u32[]{:S(2)}) async-start(bf16[32,128,256]{2,1,0:T(8,128)(2,1)} %shard_map.60), calls=%async_computation | async-start | bytes 4194304 | tf_op jit(solution)/shard_map/all_to_all | solution.py:286
  126.8 5.6 %collective-permute-start.4 = (bf16[256,1024]{1,0:T(8,128)(2,1)}, bf16[256,1024]{1,0:T(8,128)(2,1)S(1)}, u32[]{:S(2)}, u32[]{:S(2)}) collective-permute-start(bf16[256,1024]{1,0:T(8,128)(2,1)} %constant_dynamic-slice_fusion.refs_2_), channel_id=1, source_target_pairs={{0,28},{4,0},{8,4},{12,8},{16,12},{20,16},{24,20},{28,24},{1,29},{... | collective-permute-start | bytes 1572872 | tf_op jit(solution)/shard_map/ppermute | solution.py:290
  132.4 11.3 %collective-permute-done.4.refs_9_ = bf16[256,1024]{1,0:T(8,128)(2,1)S(1)} collective-permute-done((bf16[256,1024]{1,0:T(8,128)(2,1)}, bf16[256,1024]{1,0:T(8,128)(2,1)S(1)}, u32[]{:S(2)}, u32[]{:S(2)}) %collective-permute-start.4) | collective-permute-done | bytes 524320 | tf_op jit(solution)/shard_map/ppermute | solution.py:290
  147.9 10.2 %collective-permute-done.5.refs_8_ = bf16[256,1024]{1,0:T(8,128)(2,1)} collective-permute-done((bf16[256,1024]{1,0:T(8,128)(2,1)S(1)}, bf16[256,1024]{1,0:T(8,128)(2,1)}, u32[]{:S(2)}, u32[]{:S(2)}) %collective-permute-start.5) | collective-permute-done | bytes 524320 | tf_op jit(solution)/shard_map/ppermute | solution.py:290
  162.6 8.7 %collective-permute-done.6.refs_7_ = bf16[256,1024]{1,0:T(8,128)(2,1)} collective-permute-done((bf16[256,1024]{1,0:T(8,128)(2,1)}, bf16[256,1024]{1,0:T(8,128)(2,1)}, u32[]{:S(2)}, u32[]{:S(2)}) %collective-permute-start.6) | collective-permute-done | bytes 524320 | tf_op jit(solution)/shard_map/ppermute | solution.py:290
  174.5 8.1 %shard_map.62 = (bf16[264,384]{1,0:T(8,128)(2,1)}, bf16[264,384]{1,0:T(8,128)(2,1)}, bf16[264,384]{1,0:T(8,128)(2,1)}, bf16[264,384]{1,0:T(8,128)(2,1)}, bf16[26...) custom-call(s32[1]{0:T(128)} %bitcast.2.me_ref, ...), custom_call_target="tpu_custom_call" | custom-call | flops 1610612736 | bytes 14680064 | tf_op jit(solution)/shard_map/pallas_call | solution.py:227
  182.5 8.5 %shard_map.63 = (bf16[256,384]{1,0:T(8,128)(2,1)}, bf16[256,384]{1,0:T(8,128)(2,1)}, bf16[256,384]{1,0:T(8,128)(2,1)}, bf16[256,384]{1,0:T(8,128)(2,1)}, bf16[25...) custom-call(s32[1]{0:T(128)} %bitcast.2.me_ref, ...), custom_call_target="tpu_custom_call" | custom-call | flops 1610612736 | bytes 14680064 | tf_op jit(solution)/shard_map/pallas_call | solution.py:227
  191.2 7.0 %shard_map.64 = (bf16[256,256]{1,0:T(8,128)(2,1)}, bf16[256,256]{1,0:T(8,128)(2,1)}, bf16[256,256]{1,0:T(8,128)(2,1)}, bf16[256,256]{1,0:T(8,128)(2,1)}, bf16[25...) custom-call(s32[1]{0:T(128)} %bitcast.2.me_ref, ...), custom_call_target="tpu_custom_call" | custom-call | flops 1073741824 | bytes 12582912 | tf_op jit(solution)/shard_map/pallas_call | solution.py:227
  208.4 4.3 %collective-permute-done.22 = bf16[256,256]{1,0:T(8,128)(2,1)S(1)} collective-permute-done((bf16[256,256]{1,0:T(8,128)(2,1)}, bf16[256,256]{1,0:T(8,128)(2,1)S(1)}, u32[]{:S(2)}, u32[]{:S(2)}) %collective-permute-start.22) | collective-permute-done | bytes 131104 | tf_op jit(solution)/shard_map/ppermute | solution.py:290
  215.8 5.8 %collective-permute-start.15 = (bf16[256,384]{1,0:T(8,128)(2,1)S(1)}, bf16[256,384]{1,0:T(8,128)(2,1)S(1)}, u32[]{:S(2)}, u32[]{:S(2)}) collective-permute-start(bf16[256,384]{1,0:T(8,128)(2,1)S(1)} %copy-done.18), channel_id=1, source_target_pairs={{0,20},{4,24},{8,28},{12,0},{16,4},{20,8},{24,12},{28,16},{1,21},{... | collective-permute-start | bytes 589832 | tf_op jit(solution)/shard_map/ppermute | solution.py:290
  226.7 18.2 %collective-permute-done.27 = bf16[256,256]{1,0:T(8,128)(2,1)S(1)} collective-permute-done((bf16[256,256]{1,0:T(8,128)(2,1)}, bf16[256,256]{1,0:T(8,128)(2,1)S(1)}, u32[]{:S(2)}, u32[]{:S(2)}) %collective-permute-start.27) | collective-permute-done | bytes 131104 | tf_op jit(solution)/shard_map/ppermute | solution.py:290
  258.6 5.4 %collective-permute-start.7 = (bf16[264,384]{1,0:T(8,128)(2,1)S(1)}, bf16[264,384]{1,0:T(8,128)(2,1)S(1)}, u32[]{:S(2)}, u32[]{:S(2)}) collective-permute-start(bf16[264,384]{1,0:T(8,128)(2,1)S(1)} %copy-done.8), channel_id=1, source_target_pairs={{0,16},{4,20},{8,24},{12,28},{16,0},{20,4},{24,8},{28,12},{1,17},{... | collective-permute-start | bytes 608264 | tf_op jit(solution)/shard_map/ppermute | solution.py:290
  271.5 12.4 %collective-permute-done.7 = bf16[264,384]{1,0:T(8,128)(2,1)S(1)} collective-permute-done((bf16[264,384]{1,0:T(8,128)(2,1)S(1)}, bf16[264,384]{1,0:T(8,128)(2,1)S(1)}, u32[]{:S(2)}, u32[]{:S(2)}) %collective-permute-start.7) | collective-permute-done | bytes 202784 | tf_op jit(solution)/shard_map/ppermute | solution.py:290
  283.9 4.5 %collective-permute-done.8 = bf16[264,384]{1,0:T(8,128)(2,1)S(1)} collective-permute-done((bf16[264,384]{1,0:T(8,128)(2,1)S(1)}, bf16[264,384]{1,0:T(8,128)(2,1)S(1)}, u32[]{:S(2)}, u32[]{:S(2)}) %collective-permute-start.8) | collective-permute-done | bytes 202784 | tf_op jit(solution)/shard_map/ppermute | solution.py:290
  290.8 20.5 %all_to_all.34 = bf16[256,8,128]{2,0,1:T(8,128)(2,1)S(1)} all-to-all(bf16[256,8,128]{2,0,1:T(8,128)(2,1)S(1)} %copy_bitcast_fusion), channel_id=1, replica_groups=mesh['x'=4,'c'=2,'z'=8,'y'=4] {'x','c'}, dimensions={1} | all-to-all | bytes 1048576 | tf_op jit(solution)/shard_map/all_to_all | solution.py:343
  311.3 5.7 %all-to-all-start.3 = ((bf16[32,128,256]{2,1,0:T(8,128)(2,1)}), bf16[32,128,256]{2,1,0:T(8,128)(2,1)S(1)}, u32[]{:S(2)}, u32[]{:S(2)}) async-start(bf16[32,128,256]{2,1,0:T(8,128)(2,1)} %get-tuple-element.35), calls=%async_computation.3 | async-start | bytes 4194304 | tf_op jit(solution)/shard_map/all_to_all | solution.py:286
  318.1 26.0 %all-to-all-done.3 = bf16[32,128,256]{2,1,0:T(8,128)(2,1)S(1)} async-done(((bf16[32,128,256]{2,1,0:T(8,128)(2,1)}), bf16[32,128,256]{2,1,0:T(8,128)(2,1)S(1)}, u32[]{:S(2)}, u32[]{:S(2)}) %all-to-all-start.3) | async-done | bytes 2097184 | tf_op jit(solution)/shard_map/all_to_all | solution.py:286
  344.1 6.5 %shard_map.65 = bf16[2048,256]{1,0:T(8,128)(2,1)} custom-call(s32[1,2048]{1,0:T(1,128)S(1)} %copy-done, bf16[4096,256]{1,0:T(8,128)(2,1)S(1)} %bitcast.16), custom_call_target="tpu_custom_call" | custom-call | flops 4294967296 | bytes 3145728 | tf_op jit(solution)/shard_map/pallas_call | solution.py:267
  (99 shorter events, 58.4 us)
Async XLA Ops:
  73.9 45.6 %all-to-all-start.1 = ((bf16[32,136,384]{2,1,0:T(8,128)(2,1)}), bf16[32,136,384]{2,1,0:T(8,128)(2,1)S(1)}, u32[]{:S(2)}, u32[]{:S(2)}) async-start(bf16[32,136,384]{2,1,0:T(8,128)(2,1)} %get-tuple-element.32), calls=%async_computation.1 | async-start | bytes 6684672 | tf_op jit(solution)/shard_map/all_to_all | solution.py:286
  80.6 51.8 %collective-permute-start = (bf16[256,1024]{1,0:T(8,128)(2,1)}, bf16[256,1024]{1,0:T(8,128)(2,1)}, u32[]{:S(2)}, u32[]{:S(2)}) collective-permute-start(bf16[256,1024]{1,0:T(8,128)(2,1)} %constant_dynamic-slice_fusion.refs_2_), channel_id=1, source_target_pairs={{0,4},{4,8},{8,12},{12,16},{16,20},{20,24},{24,28},{28,0},{1,5},{5... | collective-permute-start | bytes 1572872 | tf_op jit(solution)/shard_map/ppermute | solution.py:290
  119.5 71.5 %all-to-all-start = ((bf16[32,128,256]{2,1,0:T(8,128)(2,1)}), bf16[32,128,256]{2,1,0:T(8,128)(2,1)}, u32[]{:S(2)}, u32[]{:S(2)}) async-start(bf16[32,128,256]{2,1,0:T(8,128)(2,1)} %shard_map.60), calls=%async_computation | async-start | bytes 4194304 | tf_op jit(solution)/shard_map/all_to_all | solution.py:286
  126.8 16.9 %collective-permute-start.4 = (bf16[256,1024]{1,0:T(8,128)(2,1)}, bf16[256,1024]{1,0:T(8,128)(2,1)S(1)}, u32[]{:S(2)}, u32[]{:S(2)}) collective-permute-start(bf16[256,1024]{1,0:T(8,128)(2,1)} %constant_dynamic-slice_fusion.refs_2_), channel_id=1, source_target_pairs={{0,28},{4,0},{8,4},{12,8},{16,12},{20,16},{24,20},{28,24},{1,29},{... | collective-permute-start | bytes 1572872 | tf_op jit(solution)/shard_map/ppermute | solution.py:290
  132.4 15.5 %collective-permute-start.1 = (bf16[256,1024]{1,0:T(8,128)(2,1)}, bf16[256,1024]{1,0:T(8,128)(2,1)S(1)}, u32[]{:S(2)}, u32[]{:S(2)}) collective-permute-start(bf16[256,1024]{1,0:T(8,128)(2,1)} %collective-permute-done.refs_3_), channel_id=1, source_target_pairs={{0,4},{4,8},{8,12},{12,16},{16,20},{20,24},{24,28},{28,0},{1,5},{5... | collective-permute-start | bytes 1572872 | tf_op jit(solution)/shard_map/ppermute | solution.py:290
  144.5 13.6 %collective-permute-start.5 = (bf16[256,1024]{1,0:T(8,128)(2,1)S(1)}, bf16[256,1024]{1,0:T(8,128)(2,1)}, u32[]{:S(2)}, u32[]{:S(2)}) collective-permute-start(bf16[256,1024]{1,0:T(8,128)(2,1)S(1)} %collective-permute-done.4.refs_9_), channel_id=1, source_target_pairs={{0,28},{4,0},{8,4},{12,8},{16,12},{20,16},{24,20},{28,24},{1,29},{... | collective-permute-start | bytes 1572872 | tf_op jit(solution)/shard_map/ppermute | solution.py:290
  147.9 13.7 %collective-permute-start.2 = (bf16[256,1024]{1,0:T(8,128)(2,1)S(1)}, bf16[256,1024]{1,0:T(8,128)(2,1)}, u32[]{:S(2)}, u32[]{:S(2)}) collective-permute-start(bf16[256,1024]{1,0:T(8,128)(2,1)S(1)} %collective-permute-done.1.refs_4_), channel_id=1, source_target_pairs={{0,4},{4,8},{8,12},{12,16},{16,20},{20,24},{24,28},{28,0},{1,5},{5... | collective-permute-start | bytes 1572872 | tf_op jit(solution)/shard_map/ppermute | solution.py:290
  201.5 14.3 %collective-permute-start.23 = (bf16[256,256]{1,0:T(8,128)(2,1)}, bf16[256,256]{1,0:T(8,128)(2,1)S(1)}, u32[]{:S(2)}, u32[]{:S(2)}) collective-permute-start(bf16[256,256]{1,0:T(8,128)(2,1)} %get-tuple-element.55), channel_id=1, source_target_pairs={{0,12},{4,16},{8,20},{12,24},{16,28},{20,0},{24,4},{28,8},{1,13},{... | collective-permute-start | bytes 393224 | tf_op jit(solution)/shard_map/ppermute | solution.py:290
  203.3 18.2 %collective-permute-start.24 = (bf16[256,256]{1,0:T(8,128)(2,1)}, bf16[256,256]{1,0:T(8,128)(2,1)S(1)}, u32[]{:S(2)}, u32[]{:S(2)}) collective-permute-start(bf16[256,256]{1,0:T(8,128)(2,1)} %get-tuple-element.56), channel_id=1, source_target_pairs={{0,24},{4,28},{8,0},{12,4},{16,8},{20,12},{24,16},{28,20},{1,25},{... | collective-permute-start | bytes 393224 | tf_op jit(solution)/shard_map/ppermute | solution.py:290
  203.8 18.6 %collective-permute-start.25 = (bf16[256,256]{1,0:T(8,128)(2,1)}, bf16[256,256]{1,0:T(8,128)(2,1)S(1)}, u32[]{:S(2)}, u32[]{:S(2)}) collective-permute-start(bf16[256,256]{1,0:T(8,128)(2,1)} %get-tuple-element.57), channel_id=1, source_target_pairs={{0,8},{4,12},{8,16},{12,20},{16,24},{20,28},{24,0},{28,4},{1,9},{5... | collective-permute-start | bytes 393224 | tf_op jit(solution)/shard_map/ppermute | solution.py:290
  206.4 18.4 %collective-permute-start.26 = (bf16[256,256]{1,0:T(8,128)(2,1)}, bf16[256,256]{1,0:T(8,128)(2,1)S(1)}, u32[]{:S(2)}, u32[]{:S(2)}) collective-permute-start(bf16[256,256]{1,0:T(8,128)(2,1)} %get-tuple-element.58), channel_id=1, source_target_pairs={{0,28},{4,0},{8,4},{12,8},{16,12},{20,16},{24,20},{28,24},{1,29},{... | collective-permute-start | bytes 393224 | tf_op jit(solution)/shard_map/ppermute | solution.py:290
  212.7 32.3 %collective-permute-start.14 = (bf16[256,384]{1,0:T(8,128)(2,1)S(1)}, bf16[256,384]{1,0:T(8,128)(2,1)S(1)}, u32[]{:S(2)}, u32[]{:S(2)}) collective-permute-start(bf16[256,384]{1,0:T(8,128)(2,1)S(1)} %copy-done.19), channel_id=1, source_target_pairs={{0,16},{4,20},{8,24},{12,28},{16,0},{20,4},{24,8},{28,12},{1,17},{... | collective-permute-start | bytes 589832 | tf_op jit(solution)/shard_map/ppermute | solution.py:290
  215.8 29.6 %collective-permute-start.15 = (bf16[256,384]{1,0:T(8,128)(2,1)S(1)}, bf16[256,384]{1,0:T(8,128)(2,1)S(1)}, u32[]{:S(2)}, u32[]{:S(2)}) collective-permute-start(bf16[256,384]{1,0:T(8,128)(2,1)S(1)} %copy-done.18), channel_id=1, source_target_pairs={{0,20},{4,24},{8,28},{12,0},{16,4},{20,8},{24,12},{28,16},{1,21},{... | collective-permute-start | bytes 589832 | tf_op jit(solution)/shard_map/ppermute | solution.py:290
  221.5 25.9 %collective-permute-start.16 = (bf16[256,384]{1,0:T(8,128)(2,1)S(1)}, bf16[256,384]{1,0:T(8,128)(2,1)S(1)}, u32[]{:S(2)}, u32[]{:S(2)}) collective-permute-start(bf16[256,384]{1,0:T(8,128)(2,1)S(1)} %copy-done.17), channel_id=1, source_target_pairs={{0,12},{4,16},{8,20},{12,24},{16,28},{20,0},{24,4},{28,8},{1,13},{... | collective-permute-start | bytes 589832 | tf_op jit(solution)/shard_map/ppermute | solution.py:290
  222.5 31.6 %collective-permute-start.17 = (bf16[256,384]{1,0:T(8,128)(2,1)S(1)}, bf16[256,384]{1,0:T(8,128)(2,1)S(1)}, u32[]{:S(2)}, u32[]{:S(2)}) collective-permute-start(bf16[256,384]{1,0:T(8,128)(2,1)S(1)} %copy-done.16), channel_id=1, source_target_pairs={{0,24},{4,28},{8,0},{12,4},{16,8},{20,12},{24,16},{28,20},{1,25},{... | collective-permute-start | bytes 589832 | tf_op jit(solution)/shard_map/ppermute | solution.py:290
  224.8 20.0 %collective-permute-start.27 = (bf16[256,256]{1,0:T(8,128)(2,1)}, bf16[256,256]{1,0:T(8,128)(2,1)S(1)}, u32[]{:S(2)}, u32[]{:S(2)}) collective-permute-start(bf16[256,256]{1,0:T(8,128)(2,1)} %get-tuple-element.59), channel_id=1, source_target_pairs={{0,4},{4,8},{8,12},{12,16},{16,20},{20,24},{24,28},{28,0},{1,5},{5... | collective-permute-start | bytes 393224 | tf_op jit(solution)/shard_map/ppermute | solution.py:290
  245.4 13.2 %collective-permute-start.20 = (bf16[256,384]{1,0:T(8,128)(2,1)S(1)}, bf16[256,384]{1,0:T(8,128)(2,1)S(1)}, u32[]{:S(2)}, u32[]{:S(2)}) collective-permute-start(bf16[256,384]{1,0:T(8,128)(2,1)S(1)} %copy-done.13), channel_id=1, source_target_pairs={{0,4},{4,8},{8,12},{12,16},{16,20},{20,24},{24,28},{28,0},{1,5},{5... | collective-permute-start | bytes 589832 | tf_op jit(solution)/shard_map/ppermute | solution.py:290
  247.4 19.5 %collective-permute-start.10 = (bf16[264,384]{1,0:T(8,128)(2,1)S(1)}, bf16[264,384]{1,0:T(8,128)(2,1)S(1)}, u32[]{:S(2)}, u32[]{:S(2)}) collective-permute-start(bf16[264,384]{1,0:T(8,128)(2,1)S(1)} %copy-done.12), channel_id=1, source_target_pairs={{0,24},{4,28},{8,0},{12,4},{16,8},{20,12},{24,16},{28,20},{1,25},{... | collective-permute-start | bytes 608264 | tf_op jit(solution)/shard_map/ppermute | solution.py:290
  257.1 13.4 %collective-permute-start.12 = (bf16[264,384]{1,0:T(8,128)(2,1)S(1)}, bf16[264,384]{1,0:T(8,128)(2,1)S(1)}, u32[]{:S(2)}, u32[]{:S(2)}) collective-permute-start(bf16[264,384]{1,0:T(8,128)(2,1)S(1)} %copy-done.10), channel_id=1, source_target_pairs={{0,28},{4,0},{8,4},{12,8},{16,12},{20,16},{24,20},{28,24},{1,29},{... | collective-permute-start | bytes 608264 | tf_op jit(solution)/shard_map/ppermute | solution.py:290
  257.2 14.4 %collective-permute-start.13 = (bf16[264,384]{1,0:T(8,128)(2,1)S(1)}, bf16[264,384]{1,0:T(8,128)(2,1)S(1)}, u32[]{:S(2)}, u32[]{:S(2)}) collective-permute-start(bf16[264,384]{1,0:T(8,128)(2,1)S(1)} %copy-done.9), channel_id=1, source_target_pairs={{0,4},{4,8},{8,12},{12,16},{16,20},{20,24},{24,28},{28,0},{1,5},{5... | collective-permute-start | bytes 608264 | tf_op jit(solution)/shard_map/ppermute | solution.py:290
  258.6 25.3 %collective-permute-start.7 = (bf16[264,384]{1,0:T(8,128)(2,1)S(1)}, bf16[264,384]{1,0:T(8,128)(2,1)S(1)}, u32[]{:S(2)}, u32[]{:S(2)}) collective-permute-start(bf16[264,384]{1,0:T(8,128)(2,1)S(1)} %copy-done.8), channel_id=1, source_target_pairs={{0,16},{4,20},{8,24},{12,28},{16,0},{20,4},{24,8},{28,12},{1,17},{... | collective-permute-start | bytes 608264 | tf_op jit(solution)/shard_map/ppermute | solution.py:290
  266.9 21.4 %collective-permute-start.8 = (bf16[264,384]{1,0:T(8,128)(2,1)S(1)}, bf16[264,384]{1,0:T(8,128)(2,1)S(1)}, u32[]{:S(2)}, u32[]{:S(2)}) collective-permute-start(bf16[264,384]{1,0:T(8,128)(2,1)S(1)} %copy-done.7), channel_id=1, source_target_pairs={{0,20},{4,24},{8,28},{12,0},{16,4},{20,8},{24,12},{28,16},{1,21},{... | collective-permute-start | bytes 608264 | tf_op jit(solution)/shard_map/ppermute | solution.py:290
  267.0 22.3 %collective-permute-start.9 = (bf16[264,384]{1,0:T(8,128)(2,1)S(1)}, bf16[264,384]{1,0:T(8,128)(2,1)S(1)}, u32[]{:S(2)}, u32[]{:S(2)}) collective-permute-start(bf16[264,384]{1,0:T(8,128)(2,1)S(1)} %copy-done.6), channel_id=1, source_target_pairs={{0,12},{4,16},{8,20},{12,24},{16,28},{20,0},{24,4},{28,8},{1,13},{... | collective-permute-start | bytes 608264 | tf_op jit(solution)/shard_map/ppermute | solution.py:290
  311.3 32.8 %all-to-all-start.3 = ((bf16[32,128,256]{2,1,0:T(8,128)(2,1)}), bf16[32,128,256]{2,1,0:T(8,128)(2,1)S(1)}, u32[]{:S(2)}, u32[]{:S(2)}) async-start(bf16[32,128,256]{2,1,0:T(8,128)(2,1)} %get-tuple-element.35), calls=%async_computation.3 | async-start | bytes 4194304 | tf_op jit(solution)/shard_map/all_to_all | solution.py:286
  (27 other events, 1114.0 us)
where the time goes:
time: 351 us
  waiting for transfers between devices  138 us (39%)
  starting transfers between devices  72.8 us (21%)
  blocking collectives  67.9 us (19%)
  Pallas kernels  63.7 us (18%)
  other arithmetic  3.78 us (1%)
  local copies, waits for them, and re-layouts  3.68 us (1%)
    ppermute x28, waiting for transfers between devices, pass_on(): lax.ppermute(values, 'z', [(i, (i + distance) % NZ) for i in range(NZ)])  82.3 us
    all_to_all x3, waiting for transfers between devices, exchange(): return lax.all_to_all(values, axes, split_axis=0, concat_axis=0, tiled=True)  55.5 us
    ppermute x28, starting transfers between devices, pass_on(): lax.ppermute(values, 'z', [(i, (i + distance) % NZ) for i in range(NZ)])  55.1 us
    all_to_all x1, blocking collectives, exchange(): return lax.all_to_all(values, axes, split_axis=0, concat_axis=0, tiled=True)  47.4 us
    pallas_call x3, Pallas kernels, block_work(): pl.pallas_call(functools.partial(work_kernel, first, last), grid_spec=plt...  23.5 us
    all_to_all x1, blocking collectives, shards(): lax.all_to_all(fresh.astype(BF16), ('x', 'c'), split_axis=1, concat_axis=...  20.5 us
    pallas_call x2, Pallas kernels, prepare(): pl.pallas_call(later_prep, grid=(steps,), in_specs=[whole, point_spec], o...  20.2 us
    all_to_all x3, starting transfers between devices, exchange(): return lax.all_to_all(values, axes, split_axis=0, concat_axis=0, tiled=True)  17.7 us
  transfers between devices with their start and end apart: 31, of which 15 were waited for; matrix products, arithmetic and copies ran while one was open for 1% of the time, Pallas kernels for 7%

commit v1 on v0

--- a/solution.py
+++ b/solution.py
@@ -15,10 +15,11 @@
 NB = NZ * NY * NG
 DESTS = NG * NY
 SLOTS = NZ * MOST
-WIDTHS = (384, 384, 256)
+WIDTHS = (512, 256, 256)
 PLANE = ("x", "c", "y")
 DIGIT = 64
 GRANT = 32 * 2**20
+WHOLE = 67043328
 PAIR = 2
 PER_STEP = 4
 F32, BF16 = jnp.float32, jnp.bfloat16
@@ -150,25 +151,20 @@
     )(block_row, final_row, points)
 
 
-def work_kernel(first, last, me_ref, *refs):
-    refs = list(refs)
-    rows_ref, target_ref = refs[:2]
-    piece_refs = refs[2 : 2 + NZ]
-    part_ref = None if first else refs[2 + NZ]
-    sum_refs, result_ref, tables, packs = refs[-NZ - 3 : -3], refs[-3], refs[-2], refs[-1]
-    places = [
-        lax.rem(me_ref[0] - (pl.program_id(0) * PAIR + b) + NZ, NZ) for b in range(PAIR)
-    ]
+def block_rows(rows_ref, b):
+    rows = rows_ref[:, b * MOST : (b + 1) * MOST, :]
+    return rows.reshape(DESTS * MOST, rows_ref.shape[-1])
+
+
+def places_of(me_ref):
+    base = me_ref[0] + NZ - pl.program_id(0) * PAIR
+    return [lax.rem(base - b, NZ) for b in range(PAIR)]
+
+
+def sums_kernel(first, me_ref, rows_ref, target_ref, *refs):
+    sum_refs, packs = refs[:NZ], refs[NZ]
     for b in range(PAIR):
-        for i in range(NZ):
-
-            @pl.when(places[b] == i)
-            def _(b=b, i=i):
-                tables[b] = piece_refs[i][...]
-
-    for b in range(PAIR):
-        rows = rows_ref[:, b * MOST : (b + 1) * MOST, :].reshape(DESTS * MOST, rows_ref.shape[-1])
-        table = tables[b]
+        rows = block_rows(rows_ref, b)
         onehot = jnp.where(
             lax.broadcasted_iota(jnp.int32, (BS, DESTS * MOST), 0) == target_ref[b], 1.0, 0.0
         ).astype(BF16)
@@ -183,6 +179,28 @@
             digits = jnp.where(which == 0, low, jnp.where(which == 1, high, 0.0))
             blank = jnp.zeros((8, sums.shape[1] - BS), F32)
             packs[b, BS : BS + 8] = jnp.concatenate([digits, blank], axis=1).astype(BF16)
+    for b, place in enumerate(places_of(me_ref)):
+        for i in range(NZ):
+
+            @pl.when(place == i)
+            def _(b=b, i=i):
+                sum_refs[i][...] = packs[b]
+
+
+def distance_kernel(first, last, me_ref, rows_ref, *refs):
+    piece_refs = refs[:NZ]
+    part_ref = None if first else refs[NZ]
+    result_ref, tables = refs[-2], refs[-1]
+    for b, place in enumerate(places_of(me_ref)):
+        for i in range(NZ):
+
+            @pl.when(place == i)
+            def _(b=b, i=i):
+                tables[b] = piece_refs[i][...]
+
+    for b in range(PAIR):
+        rows = block_rows(rows_ref, b)
+        table = tables[b]
         cross = nt_dot(rows, table)
         wide = rows.astype(F32)
         row_norm = jnp.sum(wide * wide, axis=1, keepdims=True)
@@ -197,46 +215,62 @@
             result_ref[:, b * MOST : (b + 1) * MOST, :] = total.reshape(DESTS, MOST, BS)
         else:
             result_ref[b] = total
-    for b in range(PAIR):
-        for i in range(NZ):
-
-            @pl.when(places[b] == i)
-            def _(b=b, i=i):
-                sum_refs[i][...] = packs[b]
-
-
-def block_work(me, rows, pieces, target, part, start, last):
+
+
+def both_kernel(first, me_ref, rows_ref, target_ref, *refs):
+    inputs = refs[: NZ if first else NZ + 1]
+    outputs = refs[len(inputs) :]
+    sum_refs, result_ref, packs, tables = outputs[:NZ], outputs[NZ], outputs[-2], outputs[-1]
+    distance_kernel(first, False, me_ref, rows_ref, *inputs, result_ref, tables)
+    sums_kernel(first, me_ref, rows_ref, target_ref, *sum_refs, packs)
+
+
+def block_work(me, rows, pieces, target, part, start, kind):
     width = rows.shape[-1]
-    first = part is None
+    first, last = part is None, kind == "distances"
     taken = DESTS * MOST
-    tall = BS + 8 if first else BS
+    tall = BS + 8 if first and kind == "both" else BS
     row_spec = pl.BlockSpec((DESTS, PAIR * MOST, width), lambda k, me: (0, k, 0))
     part_spec = pl.BlockSpec((PAIR, taken, BS), lambda k, me: (k, 0, 0))
-    in_specs = [row_spec, pl.BlockSpec((PAIR, 1, taken), lambda k, me: (k, 0, 0))]
-    in_specs += [pl.BlockSpec((BS, width), lambda k, me: (0, start // width))] * NZ
-    operands = [rows, target, *pieces]
-    if not first:
-        in_specs.append(part_spec)
-        operands.append(part)
-    if last:
-        result_spec = pl.BlockSpec((DESTS, PAIR * MOST, BS), lambda k, me: (0, k, 0))
-        result_shape = jax.ShapeDtypeStruct((DESTS, SLOTS, BS), BF16)
-    else:
-        result_spec = part_spec
-        result_shape = jax.ShapeDtypeStruct((NZ, taken, BS), F32)
+    operands, in_specs = [rows], [row_spec]
+    out_shape, out_specs, scratch = [], [], []
+    if kind != "distances":
+        operands.append(target)
+        in_specs.append(pl.BlockSpec((PAIR, 1, taken), lambda k, me: (k, 0, 0)))
+        out_shape += [jax.ShapeDtypeStruct((tall, width), BF16)] * NZ
+        out_specs += [pl.BlockSpec((tall, width), lambda k, me: (0, 0))] * NZ
+        scratch.append(pltpu.VMEM((PAIR, tall, width), BF16))
+    if kind != "sums":
+        operands += pieces
+        in_specs += [pl.BlockSpec((BS, width), lambda k, me: (0, start // width))] * NZ
+        scratch.append(pltpu.VMEM((PAIR, BS, width), BF16))
+        if not first:
+            operands.append(part)
+            in_specs.append(part_spec)
+        if last:
+            out_shape.append(jax.ShapeDtypeStruct((DESTS, SLOTS, BS), BF16))
+            out_specs.append(pl.BlockSpec((DESTS, PAIR * MOST, BS), lambda k, me: (0, k, 0)))
+        else:
+            out_shape.append(jax.ShapeDtypeStruct((NZ, taken, BS), F32))
+            out_specs.append(part_spec)
+    kernel = {
+        "both": functools.partial(both_kernel, first),
+        "sums": functools.partial(sums_kernel, False),
+        "distances": functools.partial(distance_kernel, first, True),
+    }[kind]
     return pl.pallas_call(
-        functools.partial(work_kernel, first, last),
+        kernel,
         grid_spec=pltpu.PrefetchScalarGridSpec(
             num_scalar_prefetch=1,
             grid=(NZ // PAIR,),
             in_specs=in_specs,
-            out_specs=(pl.BlockSpec((tall, width), lambda k, me: (0, 0)),) * NZ + (result_spec,),
-            scratch_shapes=[
-                pltpu.VMEM((PAIR, BS, width), BF16),
-                pltpu.VMEM((PAIR, tall, width), BF16),
-            ],
+            out_specs=out_specs,
+            scratch_shapes=scratch,
         ),
-        out_shape=(jax.ShapeDtypeStruct((tall, width), BF16),) * NZ + (result_shape,),
+        out_shape=out_shape,
+        compiler_params=pltpu.CompilerParams(
+            vmem_limit_bytes=WHOLE if kind == "both" else None
+        ),
         cost_estimate=pl.CostEstimate(
             flops=4 * NZ * taken * BS * width,
             bytes_accessed=2 * width * NZ * (taken + 2 * BS) + 8 * NZ * taken * BS,
@@ -329,12 +363,15 @@
     target = jnp.transpose(target.reshape(DESTS, NZ, MOST), (1, 0, 2))
     target = target.reshape(NZ, 1, DESTS * MOST)
     part, shares = None, []
-    for i in range(last + 1):
-        *sums, part = block_work(
-            me, arrived[i], pieces, target, part, starts[i], i == last
-        )
+    for i in range(last):
+        *sums, part = block_work(me, arrived[i], pieces, target, part, starts[i], "both")
         shares.append(sum_over_planes(sums))
+    (part,) = block_work(
+        me, arrived[last], pieces, target, part, starts[last], "distances"
+    )
     returned = exchange(part, PLANE).reshape(DESTS * SLOTS, BS)
+    sums = block_work(me, arrived[last], pieces, target, part, starts[last], "sums")
+    shares.append(sum_over_planes(sums))
     distances = pick_back(slot_row, returned)
 
     counts = shares[0][BS, :BS] + 16.0 * shares[0][BS + 1, :BS]

time: 351 us -> 364 us (1.037)
  waiting for transfers between devices: 138 us -> 178 us
  blocking collectives: 67.9 us -> 36.2 us
  starting transfers between devices: 72.8 us -> 76.8 us
    ppermute x28, waiting for transfers between devices: 82.3 us -> 106 us  [pass_on(): lax.ppermute(values, 'z', [(i, (i + distance) % NZ) for i in range(NZ)])]
    all_to_all x1 -> x0, blocking collectives: 20.5 us -> none  [shards(): lax.all_to_all(fresh.astype(BF16), ('x', 'c'), split_axis=1, concat_axis=...]
    all_to_all x3, waiting for transfers between devices: 55.5 us -> 69 us  [exchange(): return lax.all_to_all(values, axes, split_axis=0, concat_axis=0, tiled=True)]
    all_to_all x1, blocking collectives: 47.4 us -> 36.2 us  [exchange(): return lax.all_to_all(values, axes, split_axis=0, concat_axis=0, tiled=True)]
    all_to_all x0 -> x1, starting transfers between devices: none -> 5.25 us  [shards(): lax.all_to_all(fresh.astype(BF16), ('x', 'c'), split_axis=1, concat_axis=...]
    pallas_call x2, Pallas kernels: 20.2 us -> 15.6 us  [prepare(): pl.pallas_call(later_prep, grid=(steps,), in_specs=[whole, point_spec], o...]
    pallas_call x3 -> x4, Pallas kernels: 23.5 us -> 26.8 us  [block_work(): pl.pallas_call(kernel, grid_spec=pltpu.PrefetchScalarGridSpec(num_scalar_...]
  transfers between devices with their start and end apart: 31 -> 32, of which waited for: 15 -> 16; matrix products, arithmetic and copies ran while one was open for 1% -> 2% of each run, Pallas kernels for 7% -> 10%
where the time goes in v1:
time: 364 us; the launch traced here: 363 us
  waiting for transfers between devices  178 us (49%)
  starting transfers between devices  76.8 us (21%)
  Pallas kernels  62.6 us (17%)
  blocking collectives  36.2 us (10%)
  other arithmetic  6.29 us (2%)
    ppermute x28, waiting for transfers between devices, pass_on(): lax.ppermute(values, 'z', [(i, (i + distance) % NZ) for i in range(NZ)])  106 us
    all_to_all x3, waiting for transfers between devices, exchange(): return lax.all_to_all(values, axes, split_axis=0, concat_axis=0, tiled=True)  69 us
    ppermute x28, starting transfers between devices, pass_on(): lax.ppermute(values, 'z', [(i, (i + distance) % NZ) for i in range(NZ)])  52.2 us
    all_to_all x1, blocking collectives, exchange(): return lax.all_to_all(values, axes, split_axis=0, concat_axis=0, tiled=True)  36.2 us
    pallas_call x4, Pallas kernels, block_work(): pl.pallas_call(kernel, grid_spec=pltpu.PrefetchScalarGridSpec(num_scalar_...  26.8 us
    all_to_all x3, starting transfers between devices, exchange(): return lax.all_to_all(values, axes, split_axis=0, concat_axis=0, tiled=True)  19.3 us
    pallas_call x2, Pallas kernels, prepare(): pl.pallas_call(later_prep, grid=(steps,), in_specs=[whole, point_spec], o...  15.6 us
    pallas_call x1, Pallas kernels, prepare(): pl.pallas_call(first_prep, grid=(steps,), in_specs=[whole, whole, point_s...  13.7 us
  transfers between devices with their start and end apart: 32, of which 16 were waited for; matrix products, arithmetic and copies ran while one was open for 2% of the time, Pallas kernels for 10%

profile of v1, /device:TPU:1, one launch (start us, length us, event | category | flops | bytes accessed | tf_op | source)
XLA Modules:
  0.0 363.4 jit_solution(10598816814020740087)
XLA Ops:
  0.6 13.7 %shard_map.59 = (bf16[32,136,512]{2,1,0:T(8,128)(2,1)}, s32[1,2048]{1,0:T(1,128)}) custom-call(s32[1,2048]{1,0:T(1,128)} %bitcast.20, s32[1,2048]{1,0:T(1,128)} %bitcast.21, bf16[2048,1024]{1,0:T(8,128)(2,1)} %points_ref.5), custom_call_target="tpu_custom_call" | custom-call | flops 8589934592 | bytes 6291456 | tf_op jit(solution)/shard_map/pallas_call | solution.py:139
  14.3 7.8 %shard_map.61 = bf16[32,128,256]{2,1,0:T(8,128)(2,1)} custom-call(s32[1,2048]{1,0:T(1,128)} %get-tuple-element.30.slot_ref, bf16[2048,1024]{1,0:T(8,128)(2,1)} %points_ref.5), custom_call_target="tpu_custom_call" | custom-call | flops 4294967296 | bytes 3145728 | tf_op jit(solution)/shard_map/pallas_call | solution.py:130
  22.2 36.2 %all_to_all.33.rows_ref = bf16[32,128,256]{2,1,0:T(8,128)(2,1)} all-to-all(bf16[32,128,256]{2,1,0:T(8,128)(2,1)} %shard_map.61), channel_id=1, replica_groups=mesh['x'=4,'c'=2,'z'=8,'y'=4] {'x','c','y'}, dimensions={0} | all-to-all | bytes 4194304 | tf_op jit(solution)/shard_map/all_to_all | solution.py:320
  58.3 5.5 %all-to-all-start.2 = ((bf16[32,136,512]{2,1,0:T(8,128)(2,1)}), bf16[32,136,512]{2,1,0:T(8,128)(2,1)}, u32[]{:S(2)}, u32[]{:S(2)}) async-start(bf16[32,136,512]{2,1,0:T(8,128)(2,1)} %get-tuple-element.31), calls=%async_computation.2 | async-start | bytes 8912896 | tf_op jit(solution)/shard_map/all_to_all | solution.py:320
  66.7 7.8 %shard_map.60 = bf16[32,128,256]{2,1,0:T(8,128)(2,1)} custom-call(s32[1,2048]{1,0:T(1,128)} %get-tuple-element.30.slot_ref, bf16[2048,1024]{1,0:T(8,128)(2,1)} %points_ref.5), custom_call_target="tpu_custom_call" | custom-call | flops 4294967296 | bytes 3145728 | tf_op jit(solution)/shard_map/pallas_call | solution.py:130
  74.5 43.0 %all-to-all-done.2.rows_ref = bf16[32,136,512]{2,1,0:T(8,128)(2,1)} async-done(((bf16[32,136,512]{2,1,0:T(8,128)(2,1)}), bf16[32,136,512]{2,1,0:T(8,128)(2,1)}, u32[]{:S(2)}, u32[]{:S(2)}) %all-to-all-start.2) | async-done | bytes 4456480 | tf_op jit(solution)/shard_map/all_to_all | solution.py:320
  117.5 8.1 %all-to-all-start = ((bf16[32,128,256]{2,1,0:T(8,128)(2,1)}), bf16[32,128,256]{2,1,0:T(8,128)(2,1)}, u32[]{:S(2)}, u32[]{:S(2)}) async-start(bf16[32,128,256]{2,1,0:T(8,128)(2,1)} %shard_map.60), calls=%async_computation | async-start | bytes 4194304 | tf_op jit(solution)/shard_map/all_to_all | solution.py:320
  125.6 5.6 %collective-permute-start.4 = (bf16[256,1024]{1,0:T(8,128)(2,1)S(1)}, bf16[256,1024]{1,0:T(8,128)(2,1)S(1)}, u32[]{:S(2)}, u32[]{:S(2)}) collective-permute-start(bf16[256,1024]{1,0:T(8,128)(2,1)S(1)} %constant_dynamic-slice_fusion.refs_0_), channel_id=1, source_target_pairs={{0,28},{4,0},{8,4},{12,8},{16,12},{20,16},{24,20},{28,24},{1,29},{... | collective-permute-start | bytes 1572872 | tf_op jit(solution)/shard_map/ppermute | solution.py:324
  131.2 11.0 %collective-permute-done.4.refs_7_ = bf16[256,1024]{1,0:T(8,128)(2,1)S(1)} collective-permute-done((bf16[256,1024]{1,0:T(8,128)(2,1)S(1)}, bf16[256,1024]{1,0:T(8,128)(2,1)S(1)}, u32[]{:S(2)}, u32[]{:S(2)}) %collective-permute-start.4) | collective-permute-done | bytes 524320 | tf_op jit(solution)/shard_map/ppermute | solution.py:324
  145.8 10.1 %collective-permute-done.5.refs_6_ = bf16[256,1024]{1,0:T(8,128)(2,1)S(1)} collective-permute-done((bf16[256,1024]{1,0:T(8,128)(2,1)S(1)}, bf16[256,1024]{1,0:T(8,128)(2,1)S(1)}, u32[]{:S(2)}, u32[]{:S(2)}) %collective-permute-start.5) | collective-permute-done | bytes 524320 | tf_op jit(solution)/shard_map/ppermute | solution.py:324
  161.4 7.3 %collective-permute-done.6.refs_5_ = bf16[256,1024]{1,0:T(8,128)(2,1)S(1)} collective-permute-done((bf16[256,1024]{1,0:T(8,128)(2,1)S(1)}, bf16[256,1024]{1,0:T(8,128)(2,1)S(1)}, u32[]{:S(2)}, u32[]{:S(2)}) %collective-permute-start.6) | collective-permute-done | bytes 524320 | tf_op jit(solution)/shard_map/ppermute | solution.py:324
  172.9 8.9 %shard_map.62 = (bf16[264,512]{1,0:T(8,128)(2,1)}, bf16[264,512]{1,0:T(8,128)(2,1)}, bf16[264,512]{1,0:T(8,128)(2,1)}, bf16[264,512]{1,0:T(8,128)(2,1)}, bf16[26...) custom-call(s32[1]{0:T(128)} %bitcast.2.me_ref, ...), custom_call_target="tpu_custom_call" | custom-call | flops 2147483648 | bytes 16777216 | tf_op jit(solution)/shard_map/pallas_call | solution.py:261
  181.8 7.4 %shard_map.63 = (bf16[256,256]{1,0:T(8,128)(2,1)}, bf16[256,256]{1,0:T(8,128)(2,1)}, bf16[256,256]{1,0:T(8,128)(2,1)}, bf16[256,256]{1,0:T(8,128)(2,1)}, bf16[25...) custom-call(s32[1]{0:T(128)} %bitcast.2.me_ref, ...), custom_call_target="tpu_custom_call" | custom-call | flops 1073741824 | bytes 12582912 | tf_op jit(solution)/shard_map/pallas_call | solution.py:261
  196.8 4.4 %shard_map.66 = (bf16[256,256]{1,0:T(8,128)(2,1)}, bf16[256,256]{1,0:T(8,128)(2,1)}, bf16[256,256]{1,0:T(8,128)(2,1)}, bf16[256,256]{1,0:T(8,128)(2,1)}, bf16[25...) custom-call(s32[1]{0:T(128)} %bitcast.2.me_ref, ...), custom_call_target="tpu_custom_call" | custom-call | flops 1073741824 | bytes 12582912 | tf_op jit(solution)/shard_map/pallas_call | solution.py:261
  223.3 35.9 %collective-permute-done.22 = bf16[256,256]{1,0:T(8,128)(2,1)S(1)} collective-permute-done((bf16[256,256]{1,0:T(8,128)(2,1)}, bf16[256,256]{1,0:T(8,128)(2,1)S(1)}, u32[]{:S(2)}, u32[]{:S(2)}) %collective-permute-start.22) | collective-permute-done | bytes 131104 | tf_op jit(solution)/shard_map/ppermute | solution.py:324
  259.2 4.5 %collective-permute-start.26 = (bf16[256,256]{1,0:T(8,128)(2,1)}, bf16[256,256]{1,0:T(8,128)(2,1)S(1)}, u32[]{:S(2)}, u32[]{:S(2)}) collective-permute-start(bf16[256,256]{1,0:T(8,128)(2,1)} %get-tuple-element.56), channel_id=1, source_target_pairs={{0,28},{4,0},{8,4},{12,8},{16,12},{20,16},{24,20},{28,24},{1,29},{... | collective-permute-start | bytes 393224 | tf_op jit(solution)/shard_map/ppermute | solution.py:324
  276.9 9.1 %collective-permute-done.9 = bf16[264,512]{1,0:T(8,128)(2,1)S(1)} collective-permute-done((bf16[264,512]{1,0:T(8,128)(2,1)}, bf16[264,512]{1,0:T(8,128)(2,1)S(1)}, u32[]{:S(2)}, u32[]{:S(2)}) %collective-permute-start.9) | collective-permute-done | bytes 270368 | tf_op jit(solution)/shard_map/ppermute | solution.py:324
  286.1 12.5 %collective-permute-done.11 = bf16[264,512]{1,0:T(8,128)(2,1)S(1)} collective-permute-done((bf16[264,512]{1,0:T(8,128)(2,1)}, bf16[264,512]{1,0:T(8,128)(2,1)S(1)}, u32[]{:S(2)}, u32[]{:S(2)}) %collective-permute-start.11) | collective-permute-done | bytes 270368 | tf_op jit(solution)/shard_map/ppermute | solution.py:324
  298.6 8.6 %collective-permute-done.13 = bf16[264,512]{1,0:T(8,128)(2,1)S(1)} collective-permute-done((bf16[264,512]{1,0:T(8,128)(2,1)}, bf16[264,512]{1,0:T(8,128)(2,1)S(1)}, u32[]{:S(2)}, u32[]{:S(2)}) %collective-permute-start.13) | collective-permute-done | bytes 270368 | tf_op jit(solution)/shard_map/ppermute | solution.py:324
  309.5 5.2 %all-to-all-start.4 = ((bf16[256,8,128]{2,0,1:T(8,128)(2,1)}), bf16[256,8,128]{2,0,1:T(8,128)(2,1)S(1)}, u32[]{:S(2)}, u32[]{:S(2)}) async-start(bf16[256,8,128]{2,0,1:T(8,128)(2,1)} %copy_bitcast_fusion), calls=%async_computation.4 | async-start | bytes 1048576 | tf_op jit(solution)/shard_map/all_to_all | solution.py:380
  314.7 6.1 %shard_map.64 = bf16[32,128,256]{2,1,0:T(8,128)(2,1)} custom-call(s32[1]{0:T(128)} %bitcast.2.me_ref, bf16[32,128,256]{2,1,0:T(8,128)(2,1)} %all-to-all-done.rows_ref, bf16[256,1024]{1,0:T(8,128)(2,1)} %copy-done.1, bf16[256,1024]{1,0:T(8,128)(2,1)} %copy-done.2, bf16[256,1024]{1,0:T(8,128)(2,1)} %copy-done.4, bf16[256,1024]{1,0:T(8,128)(2,1)} %copy-done.6, ...), custom_call_target="tpu_custom_call" | custom-call | flops 1073741824 | bytes 12582912 | tf_op jit(solution)/shard_map/pallas_call | solution.py:261
  324.1 5.7 %all-to-all-start.3 = ((bf16[32,128,256]{2,1,0:T(8,128)(2,1)}), bf16[32,128,256]{2,1,0:T(8,128)(2,1)S(1)}, u32[]{:S(2)}, u32[]{:S(2)}) async-start(bf16[32,128,256]{2,1,0:T(8,128)(2,1)} %shard_map.64), calls=%async_computation.3 | async-start | bytes 4194304 | tf_op jit(solution)/shard_map/all_to_all | solution.py:320
  330.9 26.0 %all-to-all-done.3 = bf16[32,128,256]{2,1,0:T(8,128)(2,1)S(1)} async-done(((bf16[32,128,256]{2,1,0:T(8,128)(2,1)}), bf16[32,128,256]{2,1,0:T(8,128)(2,1)S(1)}, u32[]{:S(2)}, u32[]{:S(2)}) %all-to-all-start.3) | async-done | bytes 2097184 | tf_op jit(solution)/shard_map/all_to_all | solution.py:320
  356.9 6.5 %shard_map.65 = bf16[2048,256]{1,0:T(8,128)(2,1)} custom-call(s32[1,2048]{1,0:T(1,128)S(1)} %copy-done, bf16[4096,256]{1,0:T(8,128)(2,1)S(1)} %bitcast.16), custom_call_target="tpu_custom_call" | custom-call | flops 4294967296 | bytes 3145728 | tf_op jit(solution)/shard_map/pallas_call | solution.py:301
  (81 shorter events, 65.6 us)
Async XLA Ops:
  58.3 59.1 %all-to-all-start.2 = ((bf16[32,136,512]{2,1,0:T(8,128)(2,1)}), bf16[32,136,512]{2,1,0:T(8,128)(2,1)}, u32[]{:S(2)}, u32[]{:S(2)}) async-start(bf16[32,136,512]{2,1,0:T(8,128)(2,1)} %get-tuple-element.31), calls=%async_computation.2 | async-start | bytes 8912896 | tf_op jit(solution)/shard_map/all_to_all | solution.py:320
  65.0 66.3 %collective-permute-start = (bf16[256,1024]{1,0:T(8,128)(2,1)S(1)}, bf16[256,1024]{1,0:T(8,128)(2,1)S(1)}, u32[]{:S(2)}, u32[]{:S(2)}) collective-permute-start(bf16[256,1024]{1,0:T(8,128)(2,1)S(1)} %constant_dynamic-slice_fusion.refs_0_), channel_id=1, source_target_pairs={{0,4},{4,8},{8,12},{12,16},{16,20},{20,24},{24,28},{28,0},{1,5},{5... | collective-permute-start | bytes 1572872 | tf_op jit(solution)/shard_map/ppermute | solution.py:324
  117.5 79.3 %all-to-all-start = ((bf16[32,128,256]{2,1,0:T(8,128)(2,1)}), bf16[32,128,256]{2,1,0:T(8,128)(2,1)}, u32[]{:S(2)}, u32[]{:S(2)}) async-start(bf16[32,128,256]{2,1,0:T(8,128)(2,1)} %shard_map.60), calls=%async_computation | async-start | bytes 4194304 | tf_op jit(solution)/shard_map/all_to_all | solution.py:320
  125.6 16.6 %collective-permute-start.4 = (bf16[256,1024]{1,0:T(8,128)(2,1)S(1)}, bf16[256,1024]{1,0:T(8,128)(2,1)S(1)}, u32[]{:S(2)}, u32[]{:S(2)}) collective-permute-start(bf16[256,1024]{1,0:T(8,128)(2,1)S(1)} %constant_dynamic-slice_fusion.refs_0_), channel_id=1, source_target_pairs={{0,28},{4,0},{8,4},{12,8},{16,12},{20,16},{24,20},{28,24},{1,29},{... | collective-permute-start | bytes 1572872 | tf_op jit(solution)/shard_map/ppermute | solution.py:324
  131.2 14.5 %collective-permute-start.1 = (bf16[256,1024]{1,0:T(8,128)(2,1)S(1)}, bf16[256,1024]{1,0:T(8,128)(2,1)S(1)}, u32[]{:S(2)}, u32[]{:S(2)}) collective-permute-start(bf16[256,1024]{1,0:T(8,128)(2,1)S(1)} %collective-permute-done.refs_1_), channel_id=1, source_target_pairs={{0,4},{4,8},{8,12},{12,16},{16,20},{20,24},{24,28},{28,0},{1,5},{5... | collective-permute-start | bytes 1572872 | tf_op jit(solution)/shard_map/ppermute | solution.py:324
  191.1 14.8 %collective-permute-start.15 = (bf16[256,256]{1,0:T(8,128)(2,1)}, bf16[256,256]{1,0:T(8,128)(2,1)S(1)}, u32[]{:S(2)}, u32[]{:S(2)}) collective-permute-start(bf16[256,256]{1,0:T(8,128)(2,1)} %get-tuple-element.44), channel_id=1, source_target_pairs={{0,20},{4,24},{8,28},{12,0},{16,4},{20,8},{24,12},{28,16},{1,21},{... | collective-permute-start | bytes 393224 | tf_op jit(solution)/shard_map/ppermute | solution.py:324
  192.6 16.8 %collective-permute-start.16 = (bf16[256,256]{1,0:T(8,128)(2,1)}, bf16[256,256]{1,0:T(8,128)(2,1)S(1)}, u32[]{:S(2)}, u32[]{:S(2)}) collective-permute-start(bf16[256,256]{1,0:T(8,128)(2,1)} %get-tuple-element.45), channel_id=1, source_target_pairs={{0,12},{4,16},{8,20},{12,24},{16,28},{20,0},{24,4},{28,8},{1,13},{... | collective-permute-start | bytes 393224 | tf_op jit(solution)/shard_map/ppermute | solution.py:324
  194.4 17.7 %collective-permute-start.17 = (bf16[256,256]{1,0:T(8,128)(2,1)}, bf16[256,256]{1,0:T(8,128)(2,1)S(1)}, u32[]{:S(2)}, u32[]{:S(2)}) collective-permute-start(bf16[256,256]{1,0:T(8,128)(2,1)} %get-tuple-element.46), channel_id=1, source_target_pairs={{0,24},{4,28},{8,0},{12,4},{16,8},{20,12},{24,16},{28,20},{1,25},{... | collective-permute-start | bytes 393224 | tf_op jit(solution)/shard_map/ppermute | solution.py:324
  195.5 19.9 %collective-permute-start.18 = (bf16[256,256]{1,0:T(8,128)(2,1)}, bf16[256,256]{1,0:T(8,128)(2,1)S(1)}, u32[]{:S(2)}, u32[]{:S(2)}) collective-permute-start(bf16[256,256]{1,0:T(8,128)(2,1)} %get-tuple-element.47), channel_id=1, source_target_pairs={{0,8},{4,12},{8,16},{12,20},{16,24},{20,28},{24,0},{28,4},{1,9},{5... | collective-permute-start | bytes 393224 | tf_op jit(solution)/shard_map/ppermute | solution.py:324
  201.2 14.9 %collective-permute-start.19 = (bf16[256,256]{1,0:T(8,128)(2,1)}, bf16[256,256]{1,0:T(8,128)(2,1)S(1)}, u32[]{:S(2)}, u32[]{:S(2)}) collective-permute-start(bf16[256,256]{1,0:T(8,128)(2,1)} %get-tuple-element.48), channel_id=1, source_target_pairs={{0,28},{4,0},{8,4},{12,8},{16,12},{20,16},{24,20},{28,24},{1,29},{... | collective-permute-start | bytes 393224 | tf_op jit(solution)/shard_map/ppermute | solution.py:324
  205.9 14.0 %collective-permute-start.20 = (bf16[256,256]{1,0:T(8,128)(2,1)}, bf16[256,256]{1,0:T(8,128)(2,1)S(1)}, u32[]{:S(2)}, u32[]{:S(2)}) collective-permute-start(bf16[256,256]{1,0:T(8,128)(2,1)} %get-tuple-element.49), channel_id=1, source_target_pairs={{0,4},{4,8},{8,12},{12,16},{16,20},{20,24},{24,28},{28,0},{1,5},{5... | collective-permute-start | bytes 393224 | tf_op jit(solution)/shard_map/ppermute | solution.py:324
  209.3 13.9 %collective-permute-start.21 = (bf16[256,256]{1,0:T(8,128)(2,1)}, bf16[256,256]{1,0:T(8,128)(2,1)S(1)}, u32[]{:S(2)}, u32[]{:S(2)}) collective-permute-start(bf16[256,256]{1,0:T(8,128)(2,1)} %get-tuple-element.51), channel_id=1, source_target_pairs={{0,16},{4,20},{8,24},{12,28},{16,0},{20,4},{24,8},{28,12},{1,17},{... | collective-permute-start | bytes 393224 | tf_op jit(solution)/shard_map/ppermute | solution.py:324
  212.1 61.3 %collective-permute-start.7 = (bf16[264,512]{1,0:T(8,128)(2,1)}, bf16[264,512]{1,0:T(8,128)(2,1)S(1)}, u32[]{:S(2)}, u32[]{:S(2)}) collective-permute-start(bf16[264,512]{1,0:T(8,128)(2,1)} %get-tuple-element.35), channel_id=1, source_target_pairs={{0,16},{4,20},{8,24},{12,28},{16,0},{20,4},{24,8},{28,12},{1,17},{... | collective-permute-start | bytes 811016 | tf_op jit(solution)/shard_map/ppermute | solution.py:324
  215.4 58.0 %collective-permute-start.8 = (bf16[264,512]{1,0:T(8,128)(2,1)}, bf16[264,512]{1,0:T(8,128)(2,1)S(1)}, u32[]{:S(2)}, u32[]{:S(2)}) collective-permute-start(bf16[264,512]{1,0:T(8,128)(2,1)} %get-tuple-element.36), channel_id=1, source_target_pairs={{0,20},{4,24},{8,28},{12,0},{16,4},{20,8},{24,12},{28,16},{1,21},{... | collective-permute-start | bytes 811016 | tf_op jit(solution)/shard_map/ppermute | solution.py:324
  216.1 43.1 %collective-permute-start.22 = (bf16[256,256]{1,0:T(8,128)(2,1)}, bf16[256,256]{1,0:T(8,128)(2,1)S(1)}, u32[]{:S(2)}, u32[]{:S(2)}) collective-permute-start(bf16[256,256]{1,0:T(8,128)(2,1)} %get-tuple-element.52), channel_id=1, source_target_pairs={{0,20},{4,24},{8,28},{12,0},{16,4},{20,8},{24,12},{28,16},{1,21},{... | collective-permute-start | bytes 393224 | tf_op jit(solution)/shard_map/ppermute | solution.py:324
  220.0 39.3 %collective-permute-start.23 = (bf16[256,256]{1,0:T(8,128)(2,1)}, bf16[256,256]{1,0:T(8,128)(2,1)S(1)}, u32[]{:S(2)}, u32[]{:S(2)}) collective-permute-start(bf16[256,256]{1,0:T(8,128)(2,1)} %get-tuple-element.53), channel_id=1, source_target_pairs={{0,12},{4,16},{8,20},{12,24},{16,28},{20,0},{24,4},{28,8},{1,13},{... | collective-permute-start | bytes 393224 | tf_op jit(solution)/shard_map/ppermute | solution.py:324
  223.3 42.1 %collective-permute-start.24 = (bf16[256,256]{1,0:T(8,128)(2,1)}, bf16[256,256]{1,0:T(8,128)(2,1)S(1)}, u32[]{:S(2)}, u32[]{:S(2)}) collective-permute-start(bf16[256,256]{1,0:T(8,128)(2,1)} %get-tuple-element.54), channel_id=1, source_target_pairs={{0,24},{4,28},{8,0},{12,4},{16,8},{20,12},{24,16},{28,20},{1,25},{... | collective-permute-start | bytes 393224 | tf_op jit(solution)/shard_map/ppermute | solution.py:324
  265.4 20.6 %collective-permute-start.9 = (bf16[264,512]{1,0:T(8,128)(2,1)}, bf16[264,512]{1,0:T(8,128)(2,1)S(1)}, u32[]{:S(2)}, u32[]{:S(2)}) collective-permute-start(bf16[264,512]{1,0:T(8,128)(2,1)} %get-tuple-element.37), channel_id=1, source_target_pairs={{0,12},{4,16},{8,20},{12,24},{16,28},{20,0},{24,4},{28,8},{1,13},{... | collective-permute-start | bytes 811016 | tf_op jit(solution)/shard_map/ppermute | solution.py:324
  269.1 17.0 %collective-permute-start.10 = (bf16[264,512]{1,0:T(8,128)(2,1)}, bf16[264,512]{1,0:T(8,128)(2,1)S(1)}, u32[]{:S(2)}, u32[]{:S(2)}) collective-permute-start(bf16[264,512]{1,0:T(8,128)(2,1)} %get-tuple-element.38), channel_id=1, source_target_pairs={{0,24},{4,28},{8,0},{12,4},{16,8},{20,12},{24,16},{28,20},{1,25},{... | collective-permute-start | bytes 811016 | tf_op jit(solution)/shard_map/ppermute | solution.py:324
  272.4 26.2 %collective-permute-start.11 = (bf16[264,512]{1,0:T(8,128)(2,1)}, bf16[264,512]{1,0:T(8,128)(2,1)S(1)}, u32[]{:S(2)}, u32[]{:S(2)}) collective-permute-start(bf16[264,512]{1,0:T(8,128)(2,1)} %get-tuple-element.39), channel_id=1, source_target_pairs={{0,8},{4,12},{8,16},{12,20},{16,24},{20,28},{24,0},{28,4},{1,9},{5... | collective-permute-start | bytes 811016 | tf_op jit(solution)/shard_map/ppermute | solution.py:324
  273.4 25.2 %collective-permute-start.12 = (bf16[264,512]{1,0:T(8,128)(2,1)}, bf16[264,512]{1,0:T(8,128)(2,1)S(1)}, u32[]{:S(2)}, u32[]{:S(2)}) collective-permute-start(bf16[264,512]{1,0:T(8,128)(2,1)} %get-tuple-element.40), channel_id=1, source_target_pairs={{0,28},{4,0},{8,4},{12,8},{16,12},{20,16},{24,20},{28,24},{1,29},{... | collective-permute-start | bytes 811016 | tf_op jit(solution)/shard_map/ppermute | solution.py:324
  273.4 33.7 %collective-permute-start.13 = (bf16[264,512]{1,0:T(8,128)(2,1)}, bf16[264,512]{1,0:T(8,128)(2,1)S(1)}, u32[]{:S(2)}, u32[]{:S(2)}) collective-permute-start(bf16[264,512]{1,0:T(8,128)(2,1)} %get-tuple-element.41), channel_id=1, source_target_pairs={{0,4},{4,8},{8,12},{12,16},{16,20},{20,24},{24,28},{28,0},{1,5},{5... | collective-permute-start | bytes 811016 | tf_op jit(solution)/shard_map/ppermute | solution.py:324
  309.5 14.6 %all-to-all-start.4 = ((bf16[256,8,128]{2,0,1:T(8,128)(2,1)}), bf16[256,8,128]{2,0,1:T(8,128)(2,1)S(1)}, u32[]{:S(2)}, u32[]{:S(2)}) async-start(bf16[256,8,128]{2,0,1:T(8,128)(2,1)} %copy_bitcast_fusion), calls=%async_computation.4 | async-start | bytes 1048576 | tf_op jit(solution)/shard_map/all_to_all | solution.py:380
  324.1 32.8 %all-to-all-start.3 = ((bf16[32,128,256]{2,1,0:T(8,128)(2,1)}), bf16[32,128,256]{2,1,0:T(8,128)(2,1)S(1)}, u32[]{:S(2)}, u32[]{:S(2)}) async-start(bf16[32,128,256]{2,1,0:T(8,128)(2,1)} %shard_map.64), calls=%async_computation.3 | async-start | bytes 4194304 | tf_op jit(solution)/shard_map/all_to_all | solution.py:320
  (18 other events, 344.2 us)

commit v2 on v0

--- a/solution.py
+++ b/solution.py
@@ -19,6 +19,7 @@
 PLANE = ("x", "c", "y")
 DIGIT = 64
 GRANT = 32 * 2**20
+WHOLE = 67043328
 PAIR = 2
 PER_STEP = 4
 F32, BF16 = jnp.float32, jnp.bfloat16
@@ -153,8 +154,9 @@
 def work_kernel(first, last, me_ref, *refs):
     refs = list(refs)
     rows_ref, target_ref = refs[:2]
-    piece_refs = refs[2 : 2 + NZ]
-    part_ref = None if first else refs[2 + NZ]
+    piece_refs = refs[2 : 3 + NZ]
+    part_ref = None if first else refs[3 + NZ]
+    far, half = NZ // 2, BS // 2
     sum_refs, result_ref, tables, packs = refs[-NZ - 3 : -3], refs[-3], refs[-2], refs[-1]
     places = [
         lax.rem(me_ref[0] - (pl.program_id(0) * PAIR + b) + NZ, NZ) for b in range(PAIR)
@@ -164,7 +166,11 @@
 
             @pl.when(places[b] == i)
             def _(b=b, i=i):
-                tables[b] = piece_refs[i][...]
+                if i == far:
+                    tables[b, :half] = piece_refs[far][...]
+                    tables[b, half:] = piece_refs[far + 1][...]
+                else:
+                    tables[b] = piece_refs[i if i < far else i + 1][...]
 
     for b in range(PAIR):
         rows = rows_ref[:, b * MOST : (b + 1) * MOST, :].reshape(DESTS * MOST, rows_ref.shape[-1])
@@ -213,7 +219,10 @@
     row_spec = pl.BlockSpec((DESTS, PAIR * MOST, width), lambda k, me: (0, k, 0))
     part_spec = pl.BlockSpec((PAIR, taken, BS), lambda k, me: (k, 0, 0))
     in_specs = [row_spec, pl.BlockSpec((PAIR, 1, taken), lambda k, me: (k, 0, 0))]
-    in_specs += [pl.BlockSpec((BS, width), lambda k, me: (0, start // width))] * NZ
+    in_specs += [
+        pl.BlockSpec((piece.shape[0], width), lambda k, me: (0, start // width))
+        for piece in pieces
+    ]
     operands = [rows, target, *pieces]
     if not first:
         in_specs.append(part_spec)
@@ -237,6 +246,7 @@
             ],
         ),
         out_shape=(jax.ShapeDtypeStruct((tall, width), BF16),) * NZ + (result_shape,),
+        compiler_params=pltpu.CompilerParams(vmem_limit_bytes=None if last else WHOLE),
         cost_estimate=pl.CostEstimate(
             flops=4 * NZ * taken * BS * width,
             bytes_accessed=2 * width * NZ * (taken + 2 * BS) + 8 * NZ * taken * BS,
@@ -292,13 +302,13 @@
 
 def gather_table(own):
     up, down, below, above = own, own, [], []
-    for step in range(1, NZ // 2 + 1):
-        up = pass_on(up, 1)
+    for _ in range(1, NZ // 2):
+        up, down = pass_on(up, 1), pass_on(down, -1)
         below.append(up)
-        if step < NZ // 2:
-            down = pass_on(down, -1)
-            above.append(down)
-    return [own, *below, *reversed(above)]
+        above.append(down)
+    half = BS // 2
+    far = [pass_on(up[:half], 1), pass_on(down[half:], -1)]
+    return [own, *below, *far, *reversed(above)]
 
 
 def sum_over_planes(sums):

time: 351 us -> 353 us (level)
  blocking collectives: 67.9 us -> 61.8 us
  starting transfers between devices: 72.8 us -> 76.7 us
    all_to_all x1, blocking collectives: 20.5 us -> 14.4 us  [shards(): lax.all_to_all(fresh.astype(BF16), ('x', 'c'), split_axis=1, concat_axis=...]
    all_to_all x3, waiting for transfers between devices: 55.5 us -> 51.5 us  [exchange(): return lax.all_to_all(values, axes, split_axis=0, concat_axis=0, tiled=True)]
    ppermute x28 -> x29, starting transfers between devices: 55.1 us -> 58.7 us  [pass_on(): lax.ppermute(values, 'z', [(i, (i + distance) % NZ) for i in range(NZ)])]
    ppermute x28 -> x29, waiting for transfers between devices: 82.3 us -> 85 us  [pass_on(): lax.ppermute(values, 'z', [(i, (i + distance) % NZ) for i in range(NZ)])]
  transfers between devices with their start and end apart: 31 -> 32, of which waited for: 15 -> 15; matrix products, arithmetic and copies ran while one was open for 1% -> 2% of each run, Pallas kernels for 7% -> 7%
where the time goes in v2:
time: 353 us; the launch traced here: 350 us
  waiting for transfers between devices  137 us (39%)
  starting transfers between devices  76.7 us (22%)
  Pallas kernels  63.7 us (18%)
  blocking collectives  61.8 us (18%)
  local copies, waits for them, and re-layouts  6.73 us (2%)
  other arithmetic  3.79 us (1%)
    ppermute x29, waiting for transfers between devices, pass_on(): lax.ppermute(values, 'z', [(i, (i + distance) % NZ) for i in range(NZ)])  85 us
    ppermute x29, starting transfers between devices, pass_on(): lax.ppermute(values, 'z', [(i, (i + distance) % NZ) for i in range(NZ)])  58.7 us
    all_to_all x3, waiting for transfers between devices, exchange(): return lax.all_to_all(values, axes, split_axis=0, concat_axis=0, tiled=True)  51.5 us
    all_to_all x1, blocking collectives, exchange(): return lax.all_to_all(values, axes, split_axis=0, concat_axis=0, tiled=True)  47.4 us
    pallas_call x3, Pallas kernels, block_work(): pl.pallas_call(functools.partial(work_kernel, first, last), grid_spec=plt...  23.6 us
    pallas_call x2, Pallas kernels, prepare(): pl.pallas_call(later_prep, grid=(steps,), in_specs=[whole, point_spec], o...  20.2 us
    all_to_all x3, starting transfers between devices, exchange(): return lax.all_to_all(values, axes, split_axis=0, concat_axis=0, tiled=True)  18 us
    all_to_all x1, blocking collectives, shards(): lax.all_to_all(fresh.astype(BF16), ('x', 'c'), split_axis=1, concat_axis=...  14.4 us
  transfers between devices with their start and end apart: 32, of which 15 were waited for; matrix products, arithmetic and copies ran while one was open for 2% of the time, Pallas kernels for 7%

profile of v2, /device:TPU:1, one launch (start us, length us, event | category | flops | bytes accessed | tf_op | source)
XLA Modules:
  0.0 350.3 jit_solution(17233350480512018981)
XLA Ops:
  0.6 13.5 %shard_map.59 = (bf16[32,136,384]{2,1,0:T(8,128)(2,1)}, s32[1,2048]{1,0:T(1,128)}) custom-call(s32[1,2048]{1,0:T(1,128)} %bitcast.20, s32[1,2048]{1,0:T(1,128)} %bitcast.21, bf16[2048,1024]{1,0:T(8,128)(2,1)} %points_ref.5), custom_call_target="tpu_custom_call" | custom-call | flops 6442450944 | bytes 4718592 | tf_op jit(solution)/shard_map/pallas_call | solution.py:139
  14.1 12.4 %shard_map.61 = bf16[32,128,384]{2,1,0:T(8,128)(2,1)} custom-call(s32[1,2048]{1,0:T(1,128)} %get-tuple-element.31.slot_ref, bf16[2048,1024]{1,0:T(8,128)(2,1)} %points_ref.5), custom_call_target="tpu_custom_call" | custom-call | flops 6442450944 | bytes 4718592 | tf_op jit(solution)/shard_map/pallas_call | solution.py:130
  26.5 47.4 %all_to_all.33.refs_0_ = bf16[32,128,384]{2,1,0:T(8,128)(2,1)} all-to-all(bf16[32,128,384]{2,1,0:T(8,128)(2,1)} %shard_map.61), channel_id=1, replica_groups=mesh['x'=4,'c'=2,'z'=8,'y'=4] {'x','c','y'}, dimensions={0} | all-to-all | bytes 6291456 | tf_op jit(solution)/shard_map/all_to_all | solution.py:296
  73.9 4.8 %all-to-all-start.1 = ((bf16[32,136,384]{2,1,0:T(8,128)(2,1)}), bf16[32,136,384]{2,1,0:T(8,128)(2,1)S(1)}, u32[]{:S(2)}, u32[]{:S(2)}) async-start(bf16[32,136,384]{2,1,0:T(8,128)(2,1)} %get-tuple-element.32), calls=%async_computation.1 | async-start | bytes 6684672 | tf_op jit(solution)/shard_map/all_to_all | solution.py:296
  86.2 7.8 %shard_map.60 = bf16[32,128,256]{2,1,0:T(8,128)(2,1)} custom-call(s32[1,2048]{1,0:T(1,128)} %get-tuple-element.31.slot_ref, bf16[2048,1024]{1,0:T(8,128)(2,1)} %points_ref.5), custom_call_target="tpu_custom_call" | custom-call | flops 4294967296 | bytes 3145728 | tf_op jit(solution)/shard_map/pallas_call | solution.py:130
  94.0 25.5 %all-to-all-done.1.refs_0_ = bf16[32,136,384]{2,1,0:T(8,128)(2,1)S(1)} async-done(((bf16[32,136,384]{2,1,0:T(8,128)(2,1)}), bf16[32,136,384]{2,1,0:T(8,128)(2,1)S(1)}, u32[]{:S(2)}, u32[]{:S(2)}) %all-to-all-start.1) | async-done | bytes 3342368 | tf_op jit(solution)/shard_map/all_to_all | solution.py:296
  119.5 7.2 %all-to-all-start = ((bf16[32,128,256]{2,1,0:T(8,128)(2,1)}), bf16[32,128,256]{2,1,0:T(8,128)(2,1)}, u32[]{:S(2)}, u32[]{:S(2)}) async-start(bf16[32,128,256]{2,1,0:T(8,128)(2,1)} %shard_map.60), calls=%async_computation | async-start | bytes 4194304 | tf_op jit(solution)/shard_map/all_to_all | solution.py:296
  132.5 12.2 %collective-permute-done.1.refs_4_ = bf16[256,1024]{1,0:T(8,128)(2,1)S(1)} collective-permute-done((bf16[256,1024]{1,0:T(8,128)(2,1)}, bf16[256,1024]{1,0:T(8,128)(2,1)S(1)}, u32[]{:S(2)}, u32[]{:S(2)}) %collective-permute-start.1) | collective-permute-done | bytes 524320 | tf_op jit(solution)/shard_map/ppermute | solution.py:300
  147.5 11.2 %collective-permute-done.2.refs_5_ = bf16[256,1024]{1,0:T(8,128)(2,1)S(1)} collective-permute-done((bf16[256,1024]{1,0:T(8,128)(2,1)S(1)}, bf16[256,1024]{1,0:T(8,128)(2,1)S(1)}, u32[]{:S(2)}, u32[]{:S(2)}) %collective-permute-start.2) | collective-permute-done | bytes 524320 | tf_op jit(solution)/shard_map/ppermute | solution.py:300
  168.4 8.1 %shard_map.62 = (bf16[264,384]{1,0:T(8,128)(2,1)}, bf16[264,384]{1,0:T(8,128)(2,1)}, bf16[264,384]{1,0:T(8,128)(2,1)}, bf16[264,384]{1,0:T(8,128)(2,1)}, bf16[26...) custom-call(s32[1]{0:T(128)} %bitcast.2.me_ref, ...), custom_call_target="tpu_custom_call" | custom-call | flops 1610612736 | bytes 14680064 | tf_op jit(solution)/shard_map/pallas_call | solution.py:236
  176.5 8.5 %shard_map.63 = (bf16[256,384]{1,0:T(8,128)(2,1)}, bf16[256,384]{1,0:T(8,128)(2,1)}, bf16[256,384]{1,0:T(8,128)(2,1)}, bf16[256,384]{1,0:T(8,128)(2,1)}, bf16[25...) custom-call(s32[1]{0:T(128)} %bitcast.2.me_ref, ...), custom_call_target="tpu_custom_call" | custom-call | flops 1610612736 | bytes 14680064 | tf_op jit(solution)/shard_map/pallas_call | solution.py:236
  185.2 6.9 %shard_map.64 = (bf16[256,256]{1,0:T(8,128)(2,1)}, bf16[256,256]{1,0:T(8,128)(2,1)}, bf16[256,256]{1,0:T(8,128)(2,1)}, bf16[256,256]{1,0:T(8,128)(2,1)}, bf16[25...) custom-call(s32[1]{0:T(128)} %bitcast.2.me_ref, ...), custom_call_target="tpu_custom_call" | custom-call | flops 1073741824 | bytes 12582912 | tf_op jit(solution)/shard_map/pallas_call | solution.py:236
  202.0 8.5 %collective-permute-start.27 = (bf16[256,256]{1,0:T(8,128)(2,1)}, bf16[256,256]{1,0:T(8,128)(2,1)S(1)}, u32[]{:S(2)}, u32[]{:S(2)}) collective-permute-start(bf16[256,256]{1,0:T(8,128)(2,1)} %get-tuple-element.58), channel_id=1, source_target_pairs={{0,28},{4,0},{8,4},{12,8},{16,12},{20,16},{24,20},{28,24},{1,29},{... | collective-permute-start | bytes 393224 | tf_op jit(solution)/shard_map/ppermute | solution.py:300
  214.9 4.1 %collective-permute-start.17 = (bf16[256,384]{1,0:T(8,128)(2,1)S(1)}, bf16[256,384]{1,0:T(8,128)(2,1)S(1)}, u32[]{:S(2)}, u32[]{:S(2)}) collective-permute-start(bf16[256,384]{1,0:T(8,128)(2,1)S(1)} %copy-done.19), channel_id=1, source_target_pairs={{0,12},{4,16},{8,20},{12,24},{16,28},{20,0},{24,4},{28,8},{1,13},{... | collective-permute-start | bytes 589832 | tf_op jit(solution)/shard_map/ppermute | solution.py:300
  221.7 21.0 %collective-permute-done.28 = bf16[256,256]{1,0:T(8,128)(2,1)S(1)} collective-permute-done((bf16[256,256]{1,0:T(8,128)(2,1)}, bf16[256,256]{1,0:T(8,128)(2,1)S(1)}, u32[]{:S(2)}, u32[]{:S(2)}) %collective-permute-start.28) | collective-permute-done | bytes 131104 | tf_op jit(solution)/shard_map/ppermute | solution.py:300
  250.0 5.3 %collective-permute-done.19 = bf16[256,384]{1,0:T(8,128)(2,1)S(1)} collective-permute-done((bf16[256,384]{1,0:T(8,128)(2,1)S(1)}, bf16[256,384]{1,0:T(8,128)(2,1)S(1)}, u32[]{:S(2)}, u32[]{:S(2)}) %collective-permute-start.19) | collective-permute-done | bytes 196640 | tf_op jit(solution)/shard_map/ppermute | solution.py:300
  257.9 10.8 %collective-permute-done.10 = bf16[264,384]{1,0:T(8,128)(2,1)S(1)} collective-permute-done((bf16[264,384]{1,0:T(8,128)(2,1)S(1)}, bf16[264,384]{1,0:T(8,128)(2,1)S(1)}, u32[]{:S(2)}, u32[]{:S(2)}) %collective-permute-start.10) | collective-permute-done | bytes 202784 | tf_op jit(solution)/shard_map/ppermute | solution.py:300
  269.0 9.8 %collective-permute-start.9 = (bf16[264,384]{1,0:T(8,128)(2,1)S(1)}, bf16[264,384]{1,0:T(8,128)(2,1)S(1)}, u32[]{:S(2)}, u32[]{:S(2)}) collective-permute-start(bf16[264,384]{1,0:T(8,128)(2,1)S(1)} %copy-done.8), channel_id=1, source_target_pairs={{0,20},{4,24},{8,28},{12,0},{16,4},{20,8},{24,12},{28,16},{1,21},{... | collective-permute-start | bytes 608264 | tf_op jit(solution)/shard_map/ppermute | solution.py:300
  283.9 6.7 %collective-permute-done.8 = bf16[264,384]{1,0:T(8,128)(2,1)S(1)} collective-permute-done((bf16[264,384]{1,0:T(8,128)(2,1)S(1)}, bf16[264,384]{1,0:T(8,128)(2,1)S(1)}, u32[]{:S(2)}, u32[]{:S(2)}) %collective-permute-start.8) | collective-permute-done | bytes 202784 | tf_op jit(solution)/shard_map/ppermute | solution.py:300
  290.5 4.3 %collective-permute-done.9 = bf16[264,384]{1,0:T(8,128)(2,1)S(1)} collective-permute-done((bf16[264,384]{1,0:T(8,128)(2,1)S(1)}, bf16[264,384]{1,0:T(8,128)(2,1)S(1)}, u32[]{:S(2)}, u32[]{:S(2)}) %collective-permute-start.9) | collective-permute-done | bytes 202784 | tf_op jit(solution)/shard_map/ppermute | solution.py:300
  296.3 14.4 %all_to_all.34 = bf16[256,8,128]{2,0,1:T(8,128)(2,1)S(1)} all-to-all(bf16[256,8,128]{2,0,1:T(8,128)(2,1)S(1)} %copy_bitcast_fusion), channel_id=1, replica_groups=mesh['x'=4,'c'=2,'z'=8,'y'=4] {'x','c'}, dimensions={1} | all-to-all | bytes 1048576 | tf_op jit(solution)/shard_map/all_to_all | solution.py:353
  310.7 6.0 %all-to-all-start.3 = ((bf16[32,128,256]{2,1,0:T(8,128)(2,1)}), bf16[32,128,256]{2,1,0:T(8,128)(2,1)S(1)}, u32[]{:S(2)}, u32[]{:S(2)}) async-start(bf16[32,128,256]{2,1,0:T(8,128)(2,1)} %get-tuple-element.35), calls=%async_computation.3 | async-start | bytes 4194304 | tf_op jit(solution)/shard_map/all_to_all | solution.py:296
  317.8 26.0 %all-to-all-done.3 = bf16[32,128,256]{2,1,0:T(8,128)(2,1)S(1)} async-done(((bf16[32,128,256]{2,1,0:T(8,128)(2,1)}), bf16[32,128,256]{2,1,0:T(8,128)(2,1)S(1)}, u32[]{:S(2)}, u32[]{:S(2)}) %all-to-all-start.3) | async-done | bytes 2097184 | tf_op jit(solution)/shard_map/all_to_all | solution.py:296
  343.8 6.5 %shard_map.65 = bf16[2048,256]{1,0:T(8,128)(2,1)} custom-call(s32[1,2048]{1,0:T(1,128)S(1)} %copy-done, bf16[4096,256]{1,0:T(8,128)(2,1)S(1)} %bitcast.16), custom_call_target="tpu_custom_call" | custom-call | flops 4294967296 | bytes 3145728 | tf_op jit(solution)/shard_map/pallas_call | solution.py:277
  (107 shorter events, 60.4 us)
Async XLA Ops:
  73.9 45.6 %all-to-all-start.1 = ((bf16[32,136,384]{2,1,0:T(8,128)(2,1)}), bf16[32,136,384]{2,1,0:T(8,128)(2,1)S(1)}, u32[]{:S(2)}, u32[]{:S(2)}) async-start(bf16[32,136,384]{2,1,0:T(8,128)(2,1)} %get-tuple-element.32), calls=%async_computation.1 | async-start | bytes 6684672 | tf_op jit(solution)/shard_map/all_to_all | solution.py:296
  80.6 46.2 %collective-permute-start = (bf16[256,1024]{1,0:T(8,128)(2,1)}, bf16[256,1024]{1,0:T(8,128)(2,1)}, u32[]{:S(2)}, u32[]{:S(2)}) collective-permute-start(bf16[256,1024]{1,0:T(8,128)(2,1)} %constant_dynamic-slice_fusion.refs_2_), channel_id=1, source_target_pairs={{0,4},{4,8},{8,12},{12,16},{16,20},{20,24},{24,28},{28,0},{1,5},{5... | collective-permute-start | bytes 1572872 | tf_op jit(solution)/shard_map/ppermute | solution.py:300
  82.2 46.3 %collective-permute-start.4 = (bf16[256,1024]{1,0:T(8,128)(2,1)}, bf16[256,1024]{1,0:T(8,128)(2,1)}, u32[]{:S(2)}, u32[]{:S(2)}) collective-permute-start(bf16[256,1024]{1,0:T(8,128)(2,1)} %constant_dynamic-slice_fusion.refs_2_), channel_id=1, source_target_pairs={{0,28},{4,0},{8,4},{12,8},{16,12},{20,16},{24,20},{28,24},{1,29},{... | collective-permute-start | bytes 1572872 | tf_op jit(solution)/shard_map/ppermute | solution.py:300
  119.5 65.5 %all-to-all-start = ((bf16[32,128,256]{2,1,0:T(8,128)(2,1)}), bf16[32,128,256]{2,1,0:T(8,128)(2,1)}, u32[]{:S(2)}, u32[]{:S(2)}) async-start(bf16[32,128,256]{2,1,0:T(8,128)(2,1)} %shard_map.60), calls=%async_computation | async-start | bytes 4194304 | tf_op jit(solution)/shard_map/all_to_all | solution.py:296
  126.8 18.0 %collective-permute-start.1 = (bf16[256,1024]{1,0:T(8,128)(2,1)}, bf16[256,1024]{1,0:T(8,128)(2,1)S(1)}, u32[]{:S(2)}, u32[]{:S(2)}) collective-permute-start(bf16[256,1024]{1,0:T(8,128)(2,1)} %collective-permute-done.refs_3_), channel_id=1, source_target_pairs={{0,4},{4,8},{8,12},{12,16},{16,20},{20,24},{24,28},{28,0},{1,5},{5... | collective-permute-start | bytes 1572872 | tf_op jit(solution)/shard_map/ppermute | solution.py:300
  128.5 16.2 %collective-permute-start.5 = (bf16[256,1024]{1,0:T(8,128)(2,1)}, bf16[256,1024]{1,0:T(8,128)(2,1)S(1)}, u32[]{:S(2)}, u32[]{:S(2)}) collective-permute-start(bf16[256,1024]{1,0:T(8,128)(2,1)} %collective-permute-done.4.refs_10_), channel_id=1, source_target_pairs={{0,28},{4,0},{8,4},{12,8},{16,12},{20,16},{24,20},{28,24},{1,29},{... | collective-permute-start | bytes 1572872 | tf_op jit(solution)/shard_map/ppermute | solution.py:300
  195.3 18.9 %collective-permute-start.23 = (bf16[256,256]{1,0:T(8,128)(2,1)}, bf16[256,256]{1,0:T(8,128)(2,1)S(1)}, u32[]{:S(2)}, u32[]{:S(2)}) collective-permute-start(bf16[256,256]{1,0:T(8,128)(2,1)} %get-tuple-element.54), channel_id=1, source_target_pairs={{0,20},{4,24},{8,28},{12,0},{16,4},{20,8},{24,12},{28,16},{1,21},{... | collective-permute-start | bytes 393224 | tf_op jit(solution)/shard_map/ppermute | solution.py:300
  195.5 19.4 %collective-permute-start.24 = (bf16[256,256]{1,0:T(8,128)(2,1)}, bf16[256,256]{1,0:T(8,128)(2,1)S(1)}, u32[]{:S(2)}, u32[]{:S(2)}) collective-permute-start(bf16[256,256]{1,0:T(8,128)(2,1)} %get-tuple-element.55), channel_id=1, source_target_pairs={{0,12},{4,16},{8,20},{12,24},{16,28},{20,0},{24,4},{28,8},{1,13},{... | collective-permute-start | bytes 393224 | tf_op jit(solution)/shard_map/ppermute | solution.py:300
  198.6 16.3 %collective-permute-start.25 = (bf16[256,256]{1,0:T(8,128)(2,1)}, bf16[256,256]{1,0:T(8,128)(2,1)S(1)}, u32[]{:S(2)}, u32[]{:S(2)}) collective-permute-start(bf16[256,256]{1,0:T(8,128)(2,1)} %get-tuple-element.56), channel_id=1, source_target_pairs={{0,24},{4,28},{8,0},{12,4},{16,8},{20,12},{24,16},{28,20},{1,25},{... | collective-permute-start | bytes 393224 | tf_op jit(solution)/shard_map/ppermute | solution.py:300
  202.0 17.0 %collective-permute-start.26 = (bf16[256,256]{1,0:T(8,128)(2,1)}, bf16[256,256]{1,0:T(8,128)(2,1)S(1)}, u32[]{:S(2)}, u32[]{:S(2)}) collective-permute-start(bf16[256,256]{1,0:T(8,128)(2,1)} %get-tuple-element.57), channel_id=1, source_target_pairs={{0,8},{4,12},{8,16},{12,20},{16,24},{20,28},{24,0},{28,4},{1,9},{5... | collective-permute-start | bytes 393224 | tf_op jit(solution)/shard_map/ppermute | solution.py:300
  202.0 19.7 %collective-permute-start.27 = (bf16[256,256]{1,0:T(8,128)(2,1)}, bf16[256,256]{1,0:T(8,128)(2,1)S(1)}, u32[]{:S(2)}, u32[]{:S(2)}) collective-permute-start(bf16[256,256]{1,0:T(8,128)(2,1)} %get-tuple-element.58), channel_id=1, source_target_pairs={{0,28},{4,0},{8,4},{12,8},{16,12},{20,16},{24,20},{28,24},{1,29},{... | collective-permute-start | bytes 393224 | tf_op jit(solution)/shard_map/ppermute | solution.py:300
  214.3 29.4 %collective-permute-start.15 = (bf16[256,384]{1,0:T(8,128)(2,1)S(1)}, bf16[256,384]{1,0:T(8,128)(2,1)S(1)}, u32[]{:S(2)}, u32[]{:S(2)}) collective-permute-start(bf16[256,384]{1,0:T(8,128)(2,1)S(1)} %copy-done.21), channel_id=1, source_target_pairs={{0,16},{4,20},{8,24},{12,28},{16,0},{20,4},{24,8},{28,12},{1,17},{... | collective-permute-start | bytes 589832 | tf_op jit(solution)/shard_map/ppermute | solution.py:300
  214.9 30.5 %collective-permute-start.16 = (bf16[256,384]{1,0:T(8,128)(2,1)S(1)}, bf16[256,384]{1,0:T(8,128)(2,1)S(1)}, u32[]{:S(2)}, u32[]{:S(2)}) collective-permute-start(bf16[256,384]{1,0:T(8,128)(2,1)S(1)} %copy-done.20), channel_id=1, source_target_pairs={{0,20},{4,24},{8,28},{12,0},{16,4},{20,8},{24,12},{28,16},{1,21},{... | collective-permute-start | bytes 589832 | tf_op jit(solution)/shard_map/ppermute | solution.py:300
  214.9 30.5 %collective-permute-start.17 = (bf16[256,384]{1,0:T(8,128)(2,1)S(1)}, bf16[256,384]{1,0:T(8,128)(2,1)S(1)}, u32[]{:S(2)}, u32[]{:S(2)}) collective-permute-start(bf16[256,384]{1,0:T(8,128)(2,1)S(1)} %copy-done.19), channel_id=1, source_target_pairs={{0,12},{4,16},{8,20},{12,24},{16,28},{20,0},{24,4},{28,8},{1,13},{... | collective-permute-start | bytes 589832 | tf_op jit(solution)/shard_map/ppermute | solution.py:300
  219.0 30.0 %collective-permute-start.18 = (bf16[256,384]{1,0:T(8,128)(2,1)S(1)}, bf16[256,384]{1,0:T(8,128)(2,1)S(1)}, u32[]{:S(2)}, u32[]{:S(2)}) collective-permute-start(bf16[256,384]{1,0:T(8,128)(2,1)S(1)} %copy-done.18), channel_id=1, source_target_pairs={{0,24},{4,28},{8,0},{12,4},{16,8},{20,12},{24,16},{28,20},{1,25},{... | collective-permute-start | bytes 589832 | tf_op jit(solution)/shard_map/ppermute | solution.py:300
  221.7 21.0 %collective-permute-start.28 = (bf16[256,256]{1,0:T(8,128)(2,1)}, bf16[256,256]{1,0:T(8,128)(2,1)S(1)}, u32[]{:S(2)}, u32[]{:S(2)}) collective-permute-start(bf16[256,256]{1,0:T(8,128)(2,1)} %get-tuple-element.59), channel_id=1, source_target_pairs={{0,4},{4,8},{8,12},{12,16},{16,20},{20,24},{24,28},{28,0},{1,5},{5... | collective-permute-start | bytes 393224 | tf_op jit(solution)/shard_map/ppermute | solution.py:300
  245.4 23.3 %collective-permute-start.10 = (bf16[264,384]{1,0:T(8,128)(2,1)S(1)}, bf16[264,384]{1,0:T(8,128)(2,1)S(1)}, u32[]{:S(2)}, u32[]{:S(2)}) collective-permute-start(bf16[264,384]{1,0:T(8,128)(2,1)S(1)} %copy-done.14), channel_id=1, source_target_pairs={{0,12},{4,16},{8,20},{12,24},{16,28},{20,0},{24,4},{28,8},{1,13},{... | collective-permute-start | bytes 608264 | tf_op jit(solution)/shard_map/ppermute | solution.py:300
  249.0 20.0 %collective-permute-start.11 = (bf16[264,384]{1,0:T(8,128)(2,1)S(1)}, bf16[264,384]{1,0:T(8,128)(2,1)S(1)}, u32[]{:S(2)}, u32[]{:S(2)}) collective-permute-start(bf16[264,384]{1,0:T(8,128)(2,1)S(1)} %copy-done.13), channel_id=1, source_target_pairs={{0,24},{4,28},{8,0},{12,4},{16,8},{20,12},{24,16},{28,20},{1,25},{... | collective-permute-start | bytes 608264 | tf_op jit(solution)/shard_map/ppermute | solution.py:300
  255.4 26.0 %collective-permute-start.12 = (bf16[264,384]{1,0:T(8,128)(2,1)S(1)}, bf16[264,384]{1,0:T(8,128)(2,1)S(1)}, u32[]{:S(2)}, u32[]{:S(2)}) collective-permute-start(bf16[264,384]{1,0:T(8,128)(2,1)S(1)} %copy-done.12), channel_id=1, source_target_pairs={{0,8},{4,12},{8,16},{12,20},{16,24},{20,28},{24,0},{28,4},{1,9},{5... | collective-permute-start | bytes 608264 | tf_op jit(solution)/shard_map/ppermute | solution.py:300
  255.4 26.0 %collective-permute-start.13 = (bf16[264,384]{1,0:T(8,128)(2,1)S(1)}, bf16[264,384]{1,0:T(8,128)(2,1)S(1)}, u32[]{:S(2)}, u32[]{:S(2)}) collective-permute-start(bf16[264,384]{1,0:T(8,128)(2,1)S(1)} %copy-done.11), channel_id=1, source_target_pairs={{0,28},{4,0},{8,4},{12,8},{16,12},{20,16},{24,20},{28,24},{1,29},{... | collective-permute-start | bytes 608264 | tf_op jit(solution)/shard_map/ppermute | solution.py:300
  257.9 26.0 %collective-permute-start.14 = (bf16[264,384]{1,0:T(8,128)(2,1)S(1)}, bf16[264,384]{1,0:T(8,128)(2,1)S(1)}, u32[]{:S(2)}, u32[]{:S(2)}) collective-permute-start(bf16[264,384]{1,0:T(8,128)(2,1)S(1)} %copy-done.10), channel_id=1, source_target_pairs={{0,4},{4,8},{8,12},{12,16},{16,20},{20,24},{24,28},{28,0},{1,5},{5... | collective-permute-start | bytes 608264 | tf_op jit(solution)/shard_map/ppermute | solution.py:300
  268.7 21.8 %collective-permute-start.8 = (bf16[264,384]{1,0:T(8,128)(2,1)S(1)}, bf16[264,384]{1,0:T(8,128)(2,1)S(1)}, u32[]{:S(2)}, u32[]{:S(2)}) collective-permute-start(bf16[264,384]{1,0:T(8,128)(2,1)S(1)} %copy-done.9), channel_id=1, source_target_pairs={{0,16},{4,20},{8,24},{12,28},{16,0},{20,4},{24,8},{28,12},{1,17},{... | collective-permute-start | bytes 608264 | tf_op jit(solution)/shard_map/ppermute | solution.py:300
  269.0 25.8 %collective-permute-start.9 = (bf16[264,384]{1,0:T(8,128)(2,1)S(1)}, bf16[264,384]{1,0:T(8,128)(2,1)S(1)}, u32[]{:S(2)}, u32[]{:S(2)}) collective-permute-start(bf16[264,384]{1,0:T(8,128)(2,1)S(1)} %copy-done.8), channel_id=1, source_target_pairs={{0,20},{4,24},{8,28},{12,0},{16,4},{20,8},{24,12},{28,16},{1,21},{... | collective-permute-start | bytes 608264 | tf_op jit(solution)/shard_map/ppermute | solution.py:300
  310.7 33.0 %all-to-all-start.3 = ((bf16[32,128,256]{2,1,0:T(8,128)(2,1)}), bf16[32,128,256]{2,1,0:T(8,128)(2,1)S(1)}, u32[]{:S(2)}, u32[]{:S(2)}) async-start(bf16[32,128,256]{2,1,0:T(8,128)(2,1)} %get-tuple-element.35), calls=%async_computation.3 | async-start | bytes 4194304 | tf_op jit(solution)/shard_map/all_to_all | solution.py:296
  (30 other events, 1201.0 us)

commit v3 on v2

--- a/solution.py
+++ b/solution.py
@@ -21,7 +21,7 @@
 GRANT = 32 * 2**20
 WHOLE = 67043328
 PAIR = 2
-PER_STEP = 4
+PER_STEP = 8
 F32, BF16 = jnp.float32, jnp.bfloat16
 
 
@@ -106,7 +106,7 @@
     def _():
         low[...] = low_digits(slot_ref[...])
 
-    rows = PER_STEP * SLOTS
+    rows = out_ref.shape[0] * SLOTS
     pick = pick_rows(slot_ref[...], low[...], step * rows, rows)
     moved = jnp.dot(pick, points_ref[...], preferred_element_type=F32)
     out_ref[...] = moved.astype(BF16).reshape(out_ref.shape)
@@ -114,12 +114,13 @@
 
 def prepare(block_row, final_row, points, start, width, slot_row):
     npts = points.shape[0]
-    steps = DESTS // PER_STEP
+    per = PER_STEP if slot_row is None else PER_STEP // 2
+    steps = DESTS // per
     column = start // width
     whole = pl.BlockSpec((1, npts), lambda i: (0, 0))
     point_spec = pl.BlockSpec((npts, width), lambda i: (0, column))
     tall = SLOTS if slot_row is not None else SLOTS + 8
-    out_spec = pl.BlockSpec((PER_STEP, tall, width), lambda i: (i, 0, 0))
+    out_spec = pl.BlockSpec((per, tall, width), lambda i: (i, 0, 0))
     out_shape = jax.ShapeDtypeStruct((DESTS, tall, width), BF16)
     cost = pl.CostEstimate(
         flops=2 * DESTS * SLOTS * npts * width,
@@ -348,9 +349,12 @@
     distances = pick_back(slot_row, returned)
 
     counts = shares[0][BS, :BS] + 16.0 * shares[0][BS + 1, :BS]
-    total = jnp.concatenate([s[:BS] for s in shares], axis=1)
-    fresh = (total + own.astype(F32)) / (counts + 1.0)[:, None]
-    fresh = lax.all_to_all(fresh.astype(BF16), ("x", "c"), split_axis=1, concat_axis=0, tiled=True)
+    fresh = []
+    for i, share in enumerate(shares):
+        before = own[:, starts[i] : starts[i] + WIDTHS[i]].astype(F32)
+        fresh.append(((share[:BS] + before) / (counts + 1.0)[:, None]).astype(BF16))
+    fresh = jnp.concatenate([*lax.optimization_barrier(fresh[:last]), fresh[last]], axis=1)
+    fresh = lax.all_to_all(fresh, ("x", "c"), split_axis=1, concat_axis=0, tiled=True)
     return distances, fresh.astype(F32)
 
 

time: 353 us -> 346 us (0.980)
  waiting for transfers between devices: 137 us -> 109 us
  starting transfers between devices: 76.7 us -> 96.6 us
    ppermute x29, waiting for transfers between devices: 85 us -> 57.6 us  [pass_on(): lax.ppermute(values, 'z', [(i, (i + distance) % NZ) for i in range(NZ)])]
    ppermute x29, starting transfers between devices: 58.7 us -> 78.8 us  [pass_on(): lax.ppermute(values, 'z', [(i, (i + distance) % NZ) for i in range(NZ)])]
  transfers between devices with their start and end apart: 32 -> 32, of which waited for: 15 -> 15; matrix products, arithmetic and copies ran while one was open for 2% -> 2% of each run, Pallas kernels for 7% -> 9%
where the time goes in v3:
time: 346 us; the launch traced here: 345 us
  waiting for transfers between devices  109 us (32%)
  starting transfers between devices  96.6 us (28%)
  blocking collectives  63.3 us (18%)
  Pallas kernels  63 us (18%)
  local copies, waits for them, and re-layouts  6.64 us (2%)
  other arithmetic  5.19 us (2%)
    ppermute x29, starting transfers between devices, pass_on(): lax.ppermute(values, 'z', [(i, (i + distance) % NZ) for i in range(NZ)])  78.8 us
    ppermute x29, waiting for transfers between devices, pass_on(): lax.ppermute(values, 'z', [(i, (i + distance) % NZ) for i in range(NZ)])  57.6 us
    all_to_all x3, waiting for transfers between devices, exchange(): return lax.all_to_all(values, axes, split_axis=0, concat_axis=0, tiled=True)  51.5 us
    all_to_all x1, blocking collectives, exchange(): return lax.all_to_all(values, axes, split_axis=0, concat_axis=0, tiled=True)  47.4 us
    pallas_call x3, Pallas kernels, block_work(): pl.pallas_call(functools.partial(work_kernel, first, last), grid_spec=plt...  23.5 us
    pallas_call x2, Pallas kernels, prepare(): pl.pallas_call(later_prep, grid=(steps,), in_specs=[whole, point_spec], o...  20.2 us
    all_to_all x3, starting transfers between devices, exchange(): return lax.all_to_all(values, axes, split_axis=0, concat_axis=0, tiled=True)  17.8 us
    all_to_all x1, blocking collectives, shards(): lax.all_to_all(fresh, ('x', 'c'), split_axis=1, concat_axis=0, tiled=True)  15.9 us
  transfers between devices with their start and end apart: 32, of which 15 were waited for; matrix products, arithmetic and copies ran while one was open for 2% of the time, Pallas kernels for 9%

profile of v3, /device:TPU:1, one launch (start us, length us, event | category | flops | bytes accessed | tf_op | source)
XLA Modules:
  0.0 344.8 jit_solution(8681800489087729358)
XLA Ops:
  0.6 12.9 %shard_map.59 = (bf16[32,136,384]{2,1,0:T(8,128)(2,1)}, s32[1,2048]{1,0:T(1,128)}) custom-call(s32[1,2048]{1,0:T(1,128)} %bitcast.21, s32[1,2048]{1,0:T(1,128)} %bitcast.22, bf16[2048,1024]{1,0:T(8,128)(2,1)} %points_ref.5), custom_call_target="tpu_custom_call" | custom-call | flops 6442450944 | bytes 4718592 | tf_op jit(solution)/shard_map/pallas_call | solution.py:140
  13.5 12.4 %shard_map.61 = bf16[32,128,384]{2,1,0:T(8,128)(2,1)} custom-call(s32[1,2048]{1,0:T(1,128)} %get-tuple-element.33.slot_ref, bf16[2048,1024]{1,0:T(8,128)(2,1)} %points_ref.5), custom_call_target="tpu_custom_call" | custom-call | flops 6442450944 | bytes 4718592 | tf_op jit(solution)/shard_map/pallas_call | solution.py:131
  25.9 47.4 %all_to_all.33.refs_0_ = bf16[32,128,384]{2,1,0:T(8,128)(2,1)} all-to-all(bf16[32,128,384]{2,1,0:T(8,128)(2,1)} %shard_map.61), channel_id=1, replica_groups=mesh['x'=4,'c'=2,'z'=8,'y'=4] {'x','c','y'}, dimensions={0} | all-to-all | bytes 6291456 | tf_op jit(solution)/shard_map/all_to_all | solution.py:297
  73.3 4.8 %all-to-all-start.1 = ((bf16[32,136,384]{2,1,0:T(8,128)(2,1)}), bf16[32,136,384]{2,1,0:T(8,128)(2,1)S(1)}, u32[]{:S(2)}, u32[]{:S(2)}) async-start(bf16[32,136,384]{2,1,0:T(8,128)(2,1)} %get-tuple-element.34), calls=%async_computation.1 | async-start | bytes 6684672 | tf_op jit(solution)/shard_map/all_to_all | solution.py:297
  85.6 7.8 %shard_map.60 = bf16[32,128,256]{2,1,0:T(8,128)(2,1)} custom-call(s32[1,2048]{1,0:T(1,128)} %get-tuple-element.33.slot_ref, bf16[2048,1024]{1,0:T(8,128)(2,1)} %points_ref.5), custom_call_target="tpu_custom_call" | custom-call | flops 4294967296 | bytes 3145728 | tf_op jit(solution)/shard_map/pallas_call | solution.py:131
  93.4 25.5 %all-to-all-done.1.refs_0_ = bf16[32,136,384]{2,1,0:T(8,128)(2,1)S(1)} async-done(((bf16[32,136,384]{2,1,0:T(8,128)(2,1)}), bf16[32,136,384]{2,1,0:T(8,128)(2,1)S(1)}, u32[]{:S(2)}, u32[]{:S(2)}) %all-to-all-start.1) | async-done | bytes 3342368 | tf_op jit(solution)/shard_map/all_to_all | solution.py:297
  118.9 7.2 %all-to-all-start = ((bf16[32,128,256]{2,1,0:T(8,128)(2,1)}), bf16[32,128,256]{2,1,0:T(8,128)(2,1)}, u32[]{:S(2)}, u32[]{:S(2)}) async-start(bf16[32,128,256]{2,1,0:T(8,128)(2,1)} %shard_map.60), calls=%async_computation | async-start | bytes 4194304 | tf_op jit(solution)/shard_map/all_to_all | solution.py:297
  131.9 12.2 %collective-permute-done.1.refs_4_ = bf16[256,1024]{1,0:T(8,128)(2,1)S(1)} collective-permute-done((bf16[256,1024]{1,0:T(8,128)(2,1)}, bf16[256,1024]{1,0:T(8,128)(2,1)S(1)}, u32[]{:S(2)}, u32[]{:S(2)}) %collective-permute-start.1) | collective-permute-done | bytes 524320 | tf_op jit(solution)/shard_map/ppermute | solution.py:301
  146.9 11.2 %collective-permute-done.2.refs_5_ = bf16[256,1024]{1,0:T(8,128)(2,1)S(1)} collective-permute-done((bf16[256,1024]{1,0:T(8,128)(2,1)S(1)}, bf16[256,1024]{1,0:T(8,128)(2,1)S(1)}, u32[]{:S(2)}, u32[]{:S(2)}) %collective-permute-start.2) | collective-permute-done | bytes 524320 | tf_op jit(solution)/shard_map/ppermute | solution.py:301
  167.8 8.1 %shard_map.62 = (bf16[264,384]{1,0:T(8,128)(2,1)}, bf16[264,384]{1,0:T(8,128)(2,1)}, bf16[264,384]{1,0:T(8,128)(2,1)}, bf16[264,384]{1,0:T(8,128)(2,1)}, bf16[26...) custom-call(s32[1]{0:T(128)} %bitcast.2.me_ref, ...), custom_call_target="tpu_custom_call" | custom-call | flops 1610612736 | bytes 14680064 | tf_op jit(solution)/shard_map/pallas_call | solution.py:237
  175.9 4.2 %collective-permute-start.10 = (bf16[264,384]{1,0:T(8,128)(2,1)}, bf16[264,384]{1,0:T(8,128)(2,1)}, u32[]{:S(2)}, u32[]{:S(2)}) collective-permute-start(bf16[264,384]{1,0:T(8,128)(2,1)} %get-tuple-element.41), channel_id=1, source_target_pairs={{0,12},{4,16},{8,20},{12,24},{16,28},{20,0},{24,4},{28,8},{1,13},{... | collective-permute-start | bytes 608264 | tf_op jit(solution)/shard_map/ppermute | solution.py:301
  184.1 8.6 %collective-permute-start.8 = (bf16[264,384]{1,0:T(8,128)(2,1)}, bf16[264,384]{1,0:T(8,128)(2,1)}, u32[]{:S(2)}, u32[]{:S(2)}) collective-permute-start(bf16[264,384]{1,0:T(8,128)(2,1)} %get-tuple-element.39), channel_id=1, source_target_pairs={{0,16},{4,20},{8,24},{12,28},{16,0},{20,4},{24,8},{28,12},{1,17},{... | collective-permute-start | bytes 608264 | tf_op jit(solution)/shard_map/ppermute | solution.py:301
  192.7 8.5 %shard_map.63 = (bf16[256,384]{1,0:T(8,128)(2,1)}, bf16[256,384]{1,0:T(8,128)(2,1)}, bf16[256,384]{1,0:T(8,128)(2,1)}, bf16[256,384]{1,0:T(8,128)(2,1)}, bf16[25...) custom-call(s32[1]{0:T(128)} %bitcast.2.me_ref, ...), custom_call_target="tpu_custom_call" | custom-call | flops 1610612736 | bytes 14680064 | tf_op jit(solution)/shard_map/pallas_call | solution.py:237
  201.3 6.9 %shard_map.64 = (bf16[256,256]{1,0:T(8,128)(2,1)}, bf16[256,256]{1,0:T(8,128)(2,1)}, bf16[256,256]{1,0:T(8,128)(2,1)}, bf16[256,256]{1,0:T(8,128)(2,1)}, bf16[25...) custom-call(s32[1]{0:T(128)} %bitcast.2.me_ref, ...), custom_call_target="tpu_custom_call" | custom-call | flops 1073741824 | bytes 12582912 | tf_op jit(solution)/shard_map/pallas_call | solution.py:237
  208.4 9.8 %collective-permute-start.16 = (bf16[256,384]{1,0:T(8,128)(2,1)S(1)}, bf16[256,384]{1,0:T(8,128)(2,1)S(1)}, u32[]{:S(2)}, u32[]{:S(2)}) collective-permute-start(bf16[256,384]{1,0:T(8,128)(2,1)S(1)} %copy-done.14), channel_id=1, source_target_pairs={{0,20},{4,24},{8,28},{12,0},{16,4},{20,8},{24,12},{28,16},{1,21},{... | collective-permute-start | bytes 589832 | tf_op jit(solution)/shard_map/ppermute | solution.py:301
  218.1 5.4 %collective-permute-start.22 = (bf16[256,256]{1,0:T(8,128)(2,1)}, bf16[256,256]{1,0:T(8,128)(2,1)S(1)}, u32[]{:S(2)}, u32[]{:S(2)}) collective-permute-start(bf16[256,256]{1,0:T(8,128)(2,1)} %get-tuple-element.57), channel_id=1, source_target_pairs={{0,16},{4,20},{8,24},{12,28},{16,0},{20,4},{24,8},{28,12},{1,17},{... | collective-permute-start | bytes 393224 | tf_op jit(solution)/shard_map/ppermute | solution.py:301
  223.5 4.4 %collective-permute-start.23 = (bf16[256,256]{1,0:T(8,128)(2,1)}, bf16[256,256]{1,0:T(8,128)(2,1)S(1)}, u32[]{:S(2)}, u32[]{:S(2)}) collective-permute-start(bf16[256,256]{1,0:T(8,128)(2,1)} %get-tuple-element.58), channel_id=1, source_target_pairs={{0,20},{4,24},{8,28},{12,0},{16,4},{20,8},{24,12},{28,16},{1,21},{... | collective-permute-start | bytes 393224 | tf_op jit(solution)/shard_map/ppermute | solution.py:301
  229.5 10.5 %collective-permute-done.22 = bf16[256,256]{1,0:T(8,128)(2,1)S(1)} collective-permute-done((bf16[256,256]{1,0:T(8,128)(2,1)}, bf16[256,256]{1,0:T(8,128)(2,1)S(1)}, u32[]{:S(2)}, u32[]{:S(2)}) %collective-permute-start.22) | collective-permute-done | bytes 131104 | tf_op jit(solution)/shard_map/ppermute | solution.py:301
  240.5 20.2 %collective-permute-start.19 = (bf16[256,384]{1,0:T(8,128)(2,1)S(1)}, bf16[256,384]{1,0:T(8,128)(2,1)S(1)}, u32[]{:S(2)}, u32[]{:S(2)}) collective-permute-start(bf16[256,384]{1,0:T(8,128)(2,1)S(1)} %copy-done.11), channel_id=1, source_target_pairs={{0,8},{4,12},{8,16},{12,20},{16,24},{20,28},{24,0},{28,4},{1,9},{5... | collective-permute-start | bytes 589832 | tf_op jit(solution)/shard_map/ppermute | solution.py:301
  274.5 11.7 %collective-permute-done.26 = bf16[256,256]{1,0:T(8,128)(2,1)S(1)} collective-permute-done((bf16[256,256]{1,0:T(8,128)(2,1)}, bf16[256,256]{1,0:T(8,128)(2,1)S(1)}, u32[]{:S(2)}, u32[]{:S(2)}) %collective-permute-start.26) | collective-permute-done | bytes 131104 | tf_op jit(solution)/shard_map/ppermute | solution.py:301
  289.6 15.9 %all_to_all.34 = bf16[256,8,128]{2,0,1:T(8,128)(2,1)S(1)} all-to-all(bf16[256,8,128]{2,0,1:T(8,128)(2,1)S(1)} %copy_bitcast_fusion), channel_id=1, replica_groups=mesh['x'=4,'c'=2,'z'=8,'y'=4] {'x','c'}, dimensions={1} | all-to-all | bytes 1048576 | tf_op jit(solution)/shard_map/all_to_all | solution.py:357
  305.5 5.8 %all-to-all-start.3 = ((bf16[32,128,256]{2,1,0:T(8,128)(2,1)}), bf16[32,128,256]{2,1,0:T(8,128)(2,1)S(1)}, u32[]{:S(2)}, u32[]{:S(2)}) async-start(bf16[32,128,256]{2,1,0:T(8,128)(2,1)} %get-tuple-element.37), calls=%async_computation.3 | async-start | bytes 4194304 | tf_op jit(solution)/shard_map/all_to_all | solution.py:297
  312.3 26.0 %all-to-all-done.3 = bf16[32,128,256]{2,1,0:T(8,128)(2,1)S(1)} async-done(((bf16[32,128,256]{2,1,0:T(8,128)(2,1)}), bf16[32,128,256]{2,1,0:T(8,128)(2,1)S(1)}, u32[]{:S(2)}, u32[]{:S(2)}) %all-to-all-start.3) | async-done | bytes 2097184 | tf_op jit(solution)/shard_map/all_to_all | solution.py:297
  338.4 6.5 %shard_map.65 = bf16[2048,256]{1,0:T(8,128)(2,1)} custom-call(s32[1,2048]{1,0:T(1,128)S(1)} %copy-done, bf16[4096,256]{1,0:T(8,128)(2,1)S(1)} %bitcast.16), custom_call_target="tpu_custom_call" | custom-call | flops 4294967296 | bytes 3145728 | tf_op jit(solution)/shard_map/pallas_call | solution.py:278
  (94 shorter events, 50.1 us)
Async XLA Ops:
  73.3 45.6 %all-to-all-start.1 = ((bf16[32,136,384]{2,1,0:T(8,128)(2,1)}), bf16[32,136,384]{2,1,0:T(8,128)(2,1)S(1)}, u32[]{:S(2)}, u32[]{:S(2)}) async-start(bf16[32,136,384]{2,1,0:T(8,128)(2,1)} %get-tuple-element.34), calls=%async_computation.1 | async-start | bytes 6684672 | tf_op jit(solution)/shard_map/all_to_all | solution.py:297
  80.0 46.2 %collective-permute-start = (bf16[256,1024]{1,0:T(8,128)(2,1)}, bf16[256,1024]{1,0:T(8,128)(2,1)}, u32[]{:S(2)}, u32[]{:S(2)}) collective-permute-start(bf16[256,1024]{1,0:T(8,128)(2,1)} %constant_dynamic-slice_fusion.refs_2_), channel_id=1, source_target_pairs={{0,4},{4,8},{8,12},{12,16},{16,20},{20,24},{24,28},{28,0},{1,5},{5... | collective-permute-start | bytes 1572872 | tf_op jit(solution)/shard_map/ppermute | solution.py:301
  81.6 46.2 %collective-permute-start.4 = (bf16[256,1024]{1,0:T(8,128)(2,1)}, bf16[256,1024]{1,0:T(8,128)(2,1)}, u32[]{:S(2)}, u32[]{:S(2)}) collective-permute-start(bf16[256,1024]{1,0:T(8,128)(2,1)} %constant_dynamic-slice_fusion.refs_2_), channel_id=1, source_target_pairs={{0,28},{4,0},{8,4},{12,8},{16,12},{20,16},{24,20},{28,24},{1,29},{... | collective-permute-start | bytes 1572872 | tf_op jit(solution)/shard_map/ppermute | solution.py:301
  118.9 82.3 %all-to-all-start = ((bf16[32,128,256]{2,1,0:T(8,128)(2,1)}), bf16[32,128,256]{2,1,0:T(8,128)(2,1)}, u32[]{:S(2)}, u32[]{:S(2)}) async-start(bf16[32,128,256]{2,1,0:T(8,128)(2,1)} %shard_map.60), calls=%async_computation | async-start | bytes 4194304 | tf_op jit(solution)/shard_map/all_to_all | solution.py:297
  126.2 18.0 %collective-permute-start.1 = (bf16[256,1024]{1,0:T(8,128)(2,1)}, bf16[256,1024]{1,0:T(8,128)(2,1)S(1)}, u32[]{:S(2)}, u32[]{:S(2)}) collective-permute-start(bf16[256,1024]{1,0:T(8,128)(2,1)} %collective-permute-done.refs_3_), channel_id=1, source_target_pairs={{0,4},{4,8},{8,12},{12,16},{16,20},{20,24},{24,28},{28,0},{1,5},{5... | collective-permute-start | bytes 1572872 | tf_op jit(solution)/shard_map/ppermute | solution.py:301
  127.9 16.3 %collective-permute-start.5 = (bf16[256,1024]{1,0:T(8,128)(2,1)}, bf16[256,1024]{1,0:T(8,128)(2,1)S(1)}, u32[]{:S(2)}, u32[]{:S(2)}) collective-permute-start(bf16[256,1024]{1,0:T(8,128)(2,1)} %collective-permute-done.4.refs_10_), channel_id=1, source_target_pairs={{0,28},{4,0},{8,4},{12,8},{16,12},{20,16},{24,20},{28,24},{1,29},{... | collective-permute-start | bytes 1572872 | tf_op jit(solution)/shard_map/ppermute | solution.py:301
  144.1 13.9 %collective-permute-start.2 = (bf16[256,1024]{1,0:T(8,128)(2,1)S(1)}, bf16[256,1024]{1,0:T(8,128)(2,1)S(1)}, u32[]{:S(2)}, u32[]{:S(2)}) collective-permute-start(bf16[256,1024]{1,0:T(8,128)(2,1)S(1)} %collective-permute-done.1.refs_4_), channel_id=1, source_target_pairs={{0,4},{4,8},{8,12},{12,16},{16,20},{20,24},{24,28},{28,0},{1,5},{5... | collective-permute-start | bytes 1572872 | tf_op jit(solution)/shard_map/ppermute | solution.py:301
  144.9 14.6 %collective-permute-start.6 = (bf16[256,1024]{1,0:T(8,128)(2,1)S(1)}, bf16[256,1024]{1,0:T(8,128)(2,1)S(1)}, u32[]{:S(2)}, u32[]{:S(2)}) collective-permute-start(bf16[256,1024]{1,0:T(8,128)(2,1)S(1)} %collective-permute-done.5.refs_9_), channel_id=1, source_target_pairs={{0,28},{4,0},{8,4},{12,8},{16,12},{20,16},{24,20},{28,24},{1,29},{... | collective-permute-start | bytes 1572872 | tf_op jit(solution)/shard_map/ppermute | solution.py:301
  180.2 28.1 %collective-permute-start.12 = (bf16[264,384]{1,0:T(8,128)(2,1)}, bf16[264,384]{1,0:T(8,128)(2,1)}, u32[]{:S(2)}, u32[]{:S(2)}) collective-permute-start(bf16[264,384]{1,0:T(8,128)(2,1)} %get-tuple-element.43), channel_id=1, source_target_pairs={{0,8},{4,12},{8,16},{12,20},{16,24},{20,28},{24,0},{28,4},{1,9},{5... | collective-permute-start | bytes 608264 | tf_op jit(solution)/shard_map/ppermute | solution.py:301
  182.5 25.8 %collective-permute-start.13 = (bf16[264,384]{1,0:T(8,128)(2,1)}, bf16[264,384]{1,0:T(8,128)(2,1)}, u32[]{:S(2)}, u32[]{:S(2)}) collective-permute-start(bf16[264,384]{1,0:T(8,128)(2,1)} %get-tuple-element.44), channel_id=1, source_target_pairs={{0,28},{4,0},{8,4},{12,8},{16,12},{20,16},{24,20},{28,24},{1,29},{... | collective-permute-start | bytes 608264 | tf_op jit(solution)/shard_map/ppermute | solution.py:301
  184.0 34.1 %collective-permute-start.14 = (bf16[264,384]{1,0:T(8,128)(2,1)}, bf16[264,384]{1,0:T(8,128)(2,1)}, u32[]{:S(2)}, u32[]{:S(2)}) collective-permute-start(bf16[264,384]{1,0:T(8,128)(2,1)} %get-tuple-element.45), channel_id=1, source_target_pairs={{0,4},{4,8},{8,12},{12,16},{16,20},{20,24},{24,28},{28,0},{1,5},{5... | collective-permute-start | bytes 608264 | tf_op jit(solution)/shard_map/ppermute | solution.py:301
  184.1 34.0 %collective-permute-start.8 = (bf16[264,384]{1,0:T(8,128)(2,1)}, bf16[264,384]{1,0:T(8,128)(2,1)}, u32[]{:S(2)}, u32[]{:S(2)}) collective-permute-start(bf16[264,384]{1,0:T(8,128)(2,1)} %get-tuple-element.39), channel_id=1, source_target_pairs={{0,16},{4,20},{8,24},{12,28},{16,0},{20,4},{24,8},{28,12},{1,17},{... | collective-permute-start | bytes 608264 | tf_op jit(solution)/shard_map/ppermute | solution.py:301
  192.7 30.8 %collective-permute-start.9 = (bf16[264,384]{1,0:T(8,128)(2,1)}, bf16[264,384]{1,0:T(8,128)(2,1)}, u32[]{:S(2)}, u32[]{:S(2)}) collective-permute-start(bf16[264,384]{1,0:T(8,128)(2,1)} %get-tuple-element.40), channel_id=1, source_target_pairs={{0,20},{4,24},{8,28},{12,0},{16,4},{20,8},{24,12},{28,16},{1,21},{... | collective-permute-start | bytes 608264 | tf_op jit(solution)/shard_map/ppermute | solution.py:301
  208.2 52.5 %collective-permute-start.15 = (bf16[256,384]{1,0:T(8,128)(2,1)S(1)}, bf16[256,384]{1,0:T(8,128)(2,1)S(1)}, u32[]{:S(2)}, u32[]{:S(2)}) collective-permute-start(bf16[256,384]{1,0:T(8,128)(2,1)S(1)} %copy-done.15), channel_id=1, source_target_pairs={{0,16},{4,20},{8,24},{12,28},{16,0},{20,4},{24,8},{28,12},{1,17},{... | collective-permute-start | bytes 589832 | tf_op jit(solution)/shard_map/ppermute | solution.py:301
  208.4 52.3 %collective-permute-start.16 = (bf16[256,384]{1,0:T(8,128)(2,1)S(1)}, bf16[256,384]{1,0:T(8,128)(2,1)S(1)}, u32[]{:S(2)}, u32[]{:S(2)}) collective-permute-start(bf16[256,384]{1,0:T(8,128)(2,1)S(1)} %copy-done.14), channel_id=1, source_target_pairs={{0,20},{4,24},{8,28},{12,0},{16,4},{20,8},{24,12},{28,16},{1,21},{... | collective-permute-start | bytes 589832 | tf_op jit(solution)/shard_map/ppermute | solution.py:301
  218.1 44.1 %collective-permute-start.17 = (bf16[256,384]{1,0:T(8,128)(2,1)S(1)}, bf16[256,384]{1,0:T(8,128)(2,1)S(1)}, u32[]{:S(2)}, u32[]{:S(2)}) collective-permute-start(bf16[256,384]{1,0:T(8,128)(2,1)S(1)} %copy-done.13), channel_id=1, source_target_pairs={{0,12},{4,16},{8,20},{12,24},{16,28},{20,0},{24,4},{28,8},{1,13},{... | collective-permute-start | bytes 589832 | tf_op jit(solution)/shard_map/ppermute | solution.py:301
  218.1 21.9 %collective-permute-start.22 = (bf16[256,256]{1,0:T(8,128)(2,1)}, bf16[256,256]{1,0:T(8,128)(2,1)S(1)}, u32[]{:S(2)}, u32[]{:S(2)}) collective-permute-start(bf16[256,256]{1,0:T(8,128)(2,1)} %get-tuple-element.57), channel_id=1, source_target_pairs={{0,16},{4,20},{8,24},{12,28},{16,0},{20,4},{24,8},{28,12},{1,17},{... | collective-permute-start | bytes 393224 | tf_op jit(solution)/shard_map/ppermute | solution.py:301
  223.5 17.0 %collective-permute-start.23 = (bf16[256,256]{1,0:T(8,128)(2,1)}, bf16[256,256]{1,0:T(8,128)(2,1)S(1)}, u32[]{:S(2)}, u32[]{:S(2)}) collective-permute-start(bf16[256,256]{1,0:T(8,128)(2,1)} %get-tuple-element.58), channel_id=1, source_target_pairs={{0,20},{4,24},{8,28},{12,0},{16,4},{20,8},{24,12},{28,16},{1,21},{... | collective-permute-start | bytes 393224 | tf_op jit(solution)/shard_map/ppermute | solution.py:301
  240.0 23.0 %collective-permute-start.18 = (bf16[256,384]{1,0:T(8,128)(2,1)S(1)}, bf16[256,384]{1,0:T(8,128)(2,1)S(1)}, u32[]{:S(2)}, u32[]{:S(2)}) collective-permute-start(bf16[256,384]{1,0:T(8,128)(2,1)S(1)} %copy-done.12), channel_id=1, source_target_pairs={{0,24},{4,28},{8,0},{12,4},{16,8},{20,12},{24,16},{28,20},{1,25},{... | collective-permute-start | bytes 589832 | tf_op jit(solution)/shard_map/ppermute | solution.py:301
  240.5 27.4 %collective-permute-start.19 = (bf16[256,384]{1,0:T(8,128)(2,1)S(1)}, bf16[256,384]{1,0:T(8,128)(2,1)S(1)}, u32[]{:S(2)}, u32[]{:S(2)}) collective-permute-start(bf16[256,384]{1,0:T(8,128)(2,1)S(1)} %copy-done.11), channel_id=1, source_target_pairs={{0,8},{4,12},{8,16},{12,20},{16,24},{20,28},{24,0},{28,4},{1,9},{5... | collective-permute-start | bytes 589832 | tf_op jit(solution)/shard_map/ppermute | solution.py:301
  267.9 18.3 %collective-permute-start.26 = (bf16[256,256]{1,0:T(8,128)(2,1)}, bf16[256,256]{1,0:T(8,128)(2,1)S(1)}, u32[]{:S(2)}, u32[]{:S(2)}) collective-permute-start(bf16[256,256]{1,0:T(8,128)(2,1)} %get-tuple-element.61), channel_id=1, source_target_pairs={{0,8},{4,12},{8,16},{12,20},{16,24},{20,28},{24,0},{28,4},{1,9},{5... | collective-permute-start | bytes 393224 | tf_op jit(solution)/shard_map/ppermute | solution.py:301
  268.3 17.9 %collective-permute-start.27 = (bf16[256,256]{1,0:T(8,128)(2,1)}, bf16[256,256]{1,0:T(8,128)(2,1)S(1)}, u32[]{:S(2)}, u32[]{:S(2)}) collective-permute-start(bf16[256,256]{1,0:T(8,128)(2,1)} %get-tuple-element.62), channel_id=1, source_target_pairs={{0,28},{4,0},{8,4},{12,8},{16,12},{20,16},{24,20},{28,24},{1,29},{... | collective-permute-start | bytes 393224 | tf_op jit(solution)/shard_map/ppermute | solution.py:301
  272.1 16.3 %collective-permute-start.28 = (bf16[256,256]{1,0:T(8,128)(2,1)}, bf16[256,256]{1,0:T(8,128)(2,1)S(1)}, u32[]{:S(2)}, u32[]{:S(2)}) collective-permute-start(bf16[256,256]{1,0:T(8,128)(2,1)} %get-tuple-element.63), channel_id=1, source_target_pairs={{0,4},{4,8},{8,12},{12,16},{16,20},{20,24},{24,28},{28,0},{1,5},{5... | collective-permute-start | bytes 393224 | tf_op jit(solution)/shard_map/ppermute | solution.py:301
  305.5 32.8 %all-to-all-start.3 = ((bf16[32,128,256]{2,1,0:T(8,128)(2,1)}), bf16[32,128,256]{2,1,0:T(8,128)(2,1)S(1)}, u32[]{:S(2)}, u32[]{:S(2)}) async-start(bf16[32,128,256]{2,1,0:T(8,128)(2,1)} %get-tuple-element.37), calls=%async_computation.3 | async-start | bytes 4194304 | tf_op jit(solution)/shard_map/all_to_all | solution.py:297
  (24 other events, 595.2 us)
